TPU v7x, 256 devices: a whole 4x4x8 slice. The times are simulated.
256 devices in a mesh: blk: 16 (over x, z_lo, core), tp: 16 (over y, z_hi).
Axes of the slice: x: 4, y: 4, z: 8 (z_hi: 4, z_lo: 2; z = z_hi * 2 + z_lo), core: 2. Of those that a mesh axis runs over, the one named last changes fastest.
Arguments:
- residual_in: bfloat16 [8192, 5120], P('blk'), may hold values from -6 to 6
- norm_gain: bfloat16 [5120], replicated, may hold values from 0.099609375 to 1.8984375
- w_query: bfloat16 [5120, 4096], P(('blk', 'tp')), may hold values from -0.5 to 0.5
- w_key_value: bfloat16 [5120, 2048], P(('blk', 'tp')), may hold values from -0.5 to 0.5
- query_bias: bfloat16 [4096], replicated, may hold values from -3 to 3
- key_value_bias: bfloat16 [2048], replicated, may hold values from -3 to 3
- w_output: bfloat16 [4096, 5120], P(None, ('blk', 'tp')), may hold values from -0.09375 to 0.09375
- device_map: int32 [256], replicated, may hold values from 0 to 255, each once
- positions: int32 [8192], P('blk'), may hold values from 0 to 10238, as said below
- segments: int32 [8192], P('blk'), may hold values from 0 to 1, as said below
Outputs:
- output: bfloat16 [8192, 5120], P('blk', 'tp')
Inputs may be any that keep to these rules, and one draw needn't show every extreme that they name: `segments`: ids never fall; both ids 0 and 1 occur; the shorter prompt holds a quarter of 512 up to 511 tokens. `positions`: a token's index within its prompt plus an offset shared by the whole prompt; the longer prompt's last token stands at 10238. `device_map`: each of 0 to 255 once.
All inputs are finite; a program needn't handle non-finite values.
Results may differ from a plain program's by a relative error of at most 0.012.
Values may be sent and summed in bfloat16 or wider, within the bound.
A program may use at most 64 MiB of HBM per device.

v0:
```python
import jax
import jax.numpy as jnp
from jax import lax
from jax.sharding import Mesh
from jax.sharding import PartitionSpec as P

D = 5120
KVH = 8
HD = 128
TP = ("tp_0", "tp_1")
BLK_TP = ("blk", "tp_0", "tp_1")


NORM_FLOOR = 0.0625
ROPE_BASE = 1000000.0
NEGATIVE_FILL = -1e30


def from_partner(block, axis, bit):
    count = lax.axis_size(axis)
    route = []
    for low in range(count):
        high = low | 1 << bit
        if high != low and high < count:
            route += [(low, high), (high, low)]
    return lax.ppermute(block, axis, route)


def side_by_side(arrays, axis, dim, along):
    both = jnp.concatenate(arrays, axis=along)
    filled, at, outs = (lax.all_gather(both, axis, axis=dim, tiled=True), 0, [])
    for a in arrays:
        outs.append(lax.slice_in_dim(filled, at, at + a.shape[along], axis=along))
        at += a.shape[along]
    return tuple(outs)


def sum_by_axis(x, axes, dim):
    if not axes:
        return x
    nearer = lax.psum_scatter(x, axes[0], scatter_dimension=dim, tiled=True)
    return sum_by_axis(nearer, axes[1:], dim)


def rope_tables(positions, head_width):
    half_width = head_width // 2
    frequency = ROPE_BASE ** (-(jnp.arange(half_width, dtype=jnp.float32) * 2.0) / head_width)
    angles = positions.astype(jnp.float32)[:, None] * frequency[None, :]
    angles = jnp.concatenate([angles, angles], axis=1)
    return (jnp.cos(angles), jnp.sin(angles))


def rotate(values, cosine_table, sine_table):
    half_width = values.shape[-1] // 2
    turned = jnp.concatenate([-values[..., half_width:], values[..., :half_width]], axis=-1)
    return values * cosine_table[:, None, :] + turned * sine_table[:, None, :]


def join_pair(mine_cols, partner, is_lower):
    return jnp.where(
        is_lower,
        jnp.concatenate([mine_cols, partner], axis=1),
        jnp.concatenate([partner, mine_cols], axis=1),
    )


def per_device(
    residual_in,
    norm_gain,
    w_query,
    w_key_value,
    query_bias,
    key_value_bias,
    w_output,
    device_map,
    positions,
    segments,
):
    tp_count = lax.axis_size(TP)
    tp_index = lax.axis_index(TP)
    blk_index = lax.axis_index("blk")
    local_tokens = residual_in.shape[0]
    shard_rows = w_query.shape[0]
    kv_group = tp_count // KVH
    floats = residual_in.astype(jnp.float32)
    square = jnp.maximum(jnp.mean(floats * floats, axis=1, keepdims=True), NORM_FLOOR)
    normed = (floats * lax.rsqrt(square) * norm_gain.astype(jnp.float32)).astype(jnp.bfloat16)
    ordered = jnp.take(
        normed.reshape(local_tokens, device_map.shape[0], shard_rows), device_map, axis=1
    ).reshape(local_tokens, D)
    moved_query, moved_pairs = (
        lax.all_to_all(w_query, TP, split_axis=1, concat_axis=0, tiled=True),
        lax.all_to_all(w_key_value, TP, split_axis=1, concat_axis=0, tiled=True),
    )
    partner = from_partner(moved_pairs, TP, 0)
    moved_pairs = join_pair(moved_pairs, partner, tp_index >> 0 & 1 == 0)
    pieces = side_by_side((moved_query, moved_pairs), "blk", 0, 1)
    queries = jnp.dot(ordered, pieces[0], preferred_element_type=jnp.float32)
    key_value = jnp.dot(ordered, pieces[1], preferred_element_type=jnp.float32)
    query_width = queries.shape[1]
    heads_here = query_width // HD
    kv_head = tp_index // kv_group
    queries = queries + lax.dynamic_slice_in_dim(
        query_bias, tp_index * query_width, query_width
    ).astype(jnp.float32)
    key_value = key_value + lax.dynamic_slice_in_dim(
        key_value_bias, kv_head * 2 * HD, 2 * HD
    ).astype(jnp.float32)
    cosine_table, sine_table = rope_tables(positions, HD)
    query_rot = rotate(
        queries.reshape(local_tokens, heads_here, HD), cosine_table, sine_table
    ).astype(jnp.bfloat16)
    key_rot = rotate(key_value[:, None, :HD], cosine_table, sine_table)[:, 0, :].astype(
        jnp.bfloat16
    )
    values = key_value[:, HD:].astype(jnp.bfloat16)
    attend_scale = HD ** (-0.5)
    row_index = blk_index * local_tokens + jnp.arange(local_tokens, dtype=jnp.int32)
    initial = (
        jnp.full((heads_here, local_tokens), NEGATIVE_FILL, jnp.float32),
        jnp.zeros((heads_here, local_tokens), jnp.float32),
        jnp.zeros((heads_here, local_tokens, HD), jnp.float32),
    )
    key_piece, value_piece, segment_piece = (
        *side_by_side((key_rot, values), "blk", 0, 1),
        lax.all_gather(segments, "blk", axis=0, tiled=True),
    )
    piece_rows = key_piece.shape[0]
    key_block_rows = 512

    def one_block(block_number, state_now):
        run_peak, run_mass, context = state_now
        block_start = block_number * key_block_rows
        key_block = lax.dynamic_slice_in_dim(key_piece, block_start, key_block_rows, 0)
        value_block = lax.dynamic_slice_in_dim(value_piece, block_start, key_block_rows, 0)
        segment_block = lax.dynamic_slice_in_dim(segment_piece, block_start, key_block_rows, 0)
        scores = (
            jnp.einsum("qhd,kd->hqk", query_rot, key_block, preferred_element_type=jnp.float32)
            * attend_scale
        )
        key_index = block_start + jnp.arange(key_block_rows, dtype=jnp.int32)
        visible = (key_index[None, :] <= row_index[:, None]) & (
            segment_block[None, :] == segments[:, None]
        )
        masked = jnp.where(visible[None], scores, NEGATIVE_FILL)
        new_peak = jnp.maximum(run_peak, jnp.max(masked, axis=2))
        factor = jnp.exp(run_peak - new_peak)
        raw_weights = jnp.where(visible[None], jnp.exp(masked - new_peak[:, :, None]), 0.0)
        run_mass = run_mass * factor + jnp.sum(raw_weights, axis=2)
        context = context * factor[:, :, None] + jnp.einsum(
            "hqk,kd->hqd",
            raw_weights.astype(jnp.bfloat16),
            value_block,
            preferred_element_type=jnp.float32,
        )
        return (new_peak, run_mass, context)

    run_peak, run_mass, context = lax.fori_loop(0, piece_rows // key_block_rows, one_block, initial)
    context_flat = (
        (context / run_mass[:, :, None])
        .transpose(1, 0, 2)
        .reshape(local_tokens, query_width)
        .astype(jnp.bfloat16)
    )
    width_out = D // tp_count
    moved_out = lax.all_to_all(w_output, TP, split_axis=0, concat_axis=1, tiled=True)
    row_terms = jnp.dot(
        context_flat,
        lax.all_gather(moved_out, "blk", axis=1, tiled=True),
        preferred_element_type=jnp.float32,
    )
    summed = sum_by_axis(row_terms.astype(jnp.bfloat16), TP, 1).astype(jnp.float32)
    residual_part = lax.dynamic_slice_in_dim(residual_in, tp_index * width_out, width_out, 1)
    return (residual_part.astype(jnp.float32) + summed).astype(jnp.bfloat16)


def solution(mesh):
    split = Mesh(mesh.devices.reshape(mesh.shape["blk"], 4, 4), ("blk", "tp_0", "tp_1"))
    placed = (
        P("blk", None),
        P(),
        P(BLK_TP, None),
        P(BLK_TP, None),
        P(),
        P(),
        P(None, BLK_TP),
        P(),
        P("blk"),
        P("blk"),
    )
    return jax.shard_map(
        per_device, mesh=split, in_specs=placed, out_specs=P("blk", TP), check_vma=False
    )
```

profile of v0, /device:TPU:6, one launch (start us, length us, event | category | flops | bytes accessed | tf_op | source)
XLA Modules:
  0.0 323.4 jit_solution(2064441790965628056)
XLA Ops:
  8.1 11.2 %all-to-all-start.1 = ((bf16[20,16,128]{2,0,1:T(8,128)(2,1)}), bf16[20,16,128]{2,0,1:T(8,128)(2,1)S(1)}, u32[]{:S(2)}, u32[]{:S(2)}) async-start(bf16[20,16,128]{2,0,1:T(8,128)(2,1)} %copy.37), calls=%async_computation.1 | async-start | bytes 196608 | tf_op jit(solution)/shard_map/all_to_all | solution.py:93
  21.1 8.7 %all-to-all-done.1 = bf16[20,16,128]{2,0,1:T(8,128)(2,1)S(1)} async-done(((bf16[20,16,128]{2,0,1:T(8,128)(2,1)}), bf16[20,16,128]{2,0,1:T(8,128)(2,1)S(1)}, u32[]{:S(2)}, u32[]{:S(2)}) %all-to-all-start.1) | async-done | bytes 81952 | tf_op jit(solution)/shard_map/all_to_all | solution.py:93
  29.8 3.5 %all-to-all-start = ((bf16[20,16,256]{2,0,1:T(8,128)(2,1)}), bf16[20,16,256]{2,0,1:T(8,128)(2,1)S(1)}, u32[]{:S(2)}, u32[]{:S(2)}) async-start(bf16[20,16,256]{2,0,1:T(8,128)(2,1)} %copy.36), calls=%async_computation | async-start | bytes 393216 | tf_op jit(solution)/shard_map/all_to_all | solution.py:92
  33.4 2.8 collective-permute-start
  36.2 6.6 %collective-permute-done = bf16[320,128]{1,0:T(8,128)(2,1)S(1)} collective-permute-done((bf16[320,128]{1,0:T(8,128)(2,1)S(1)}, bf16[320,128]{1,0:T(8,128)(2,1)S(1)}, u32[]{:S(2)}, u32[]{:S(2)}) %collective-permute-start) | collective-permute-done | bytes 81952 | tf_op jit(solution)/shard_map/ppermute | solution.py:26
  42.8 2.2 all-to-all-done
  46.0 3.7 %fusion.22 = f32[512]{0:T(512)S(1)} fusion(bf16[512,5120]{1,0:T(8,128)(2,1)} %param.12), kind=kLoop, calls=%fused_computation.33 | loop fusion | flops 7863808 | bytes 5244928 | tf_op jit(solution)/shard_map/reduce_sum | solution.py:86
  50.0 4.3 %fusion.24 = bf16[512,5120]{1,0:T(8,128)(2,1)} fusion(bf16[512,5120]{1,0:T(8,128)(2,1)S(1)} %copy-done, f32[5120]{0:T(1024)S(1)} %convert_element_type.55, f32[512]{0:T(512)S(1)} %maximum_rsqrt_fusion), kind=kLoop, calls=%fused_computation.35 | loop fusion | flops 10485760 | bytes 10508288 | tf_op jit(solution)/shard_map/convert_element_type | solution.py:87
  54.3 8.0 %copy.35 = bf16[512,5120]{0,1:T(8,128)(2,1)} copy(bf16[512,5120]{1,0:T(8,128)(2,1)} %fusion.24) | data formatting | bytes 10485760 | tf_op jit(solution)/shard_map/convert_element_type | solution.py:87
  62.4 9.0 %reshape.163 = bf16[512,256,20]{0,2,1:T(8,128)(2,1)} reshape(bf16[512,5120]{0,1:T(8,128)(2,1)} %copy.35) | data formatting | bytes 10485760 | tf_op jit(solution)/shard_map/reshape | solution.py:89
  71.3 6.4 %gather_fusion = bf16[256,512,20]{1,2,0:T(8,128)(2,1)} fusion(bf16[512,256,20]{0,2,1:T(8,128)(2,1)} %reshape.163, s32[1024]{0:T(1024)S(1)} %pad_clamp_fusion), kind=kCustom, calls=%fused_computation | custom fusion | bytes 10486784 | tf_op jit(solution)/shard_map/jit(_take)/gather | solution.py:88
  77.8 9.0 %gather.7 = bf16[512,5120]{0,1:T(8,128)(2,1)} reshape(bf16[512,256,20]{0,2,1:T(8,128)(2,1)} %bitcast.72) | data formatting | bytes 10485760 | tf_op jit(solution)/shard_map/jit(_take)/gather | solution.py:88
  88.0 5.7 %fusion.29 = f32[512,256]{0,1:T(8,128)S(1)} fusion(bf16[5120,512]{1,0:T(8,128)(2,1)} %all-gather.5.cloned.1.call-done, bf16[512,5120]{0,1:T(8,128)(2,1)} %gather.7, pred[5120]{0:T(1024)(128)(4,1)S(1)} %broadcast_in_dim.101, f32[256]{0:T(256)S(1)} %dynamic-slice_convert_fusion.1), kind=kOutput, calls=%fused_computation.42 | convolution fusion | flops 1344929792 | bytes 8394752 | tf_op jit(solution)/shard_map/dot_general | solution.py:99
  96.4 5.3 %all-to-all-start.2 = ((bf16[16,256,20]{1,2,0:T(8,128)(2,1)}), bf16[16,256,20]{1,2,0:T(8,128)(2,1)S(1)}, u32[]{:S(2)}, u32[]{:S(2)}) async-start(bf16[16,256,20]{1,2,0:T(8,128)(2,1)} %copy.46), calls=%async_computation.2 | async-start | bytes 393216 | tf_op jit(solution)/shard_map/all_to_all | solution.py:166
  101.7 17.7 %all-gather = s32[16,1,512]{2,1,0:T(1,128)S(1)} all-gather(s32[1,1,512]{2,1,0:T(1,128)S(1)} %bitcast.86), channel_id=1, replica_groups=mesh['blk'=16,'tp_0'=4,'tp_1'=4] {'blk'}, dimensions={0}, use_global_device_ids=true | all-gather | bytes 34816 | tf_op jit(solution)/shard_map/all_gather | solution.py:126
  121.4 5.8 %fusion.32 = f32[512,256]{0,1:T(8,128)S(1)} fusion(bf16[5120,512]{1,0:T(8,128)(2,1)} %all-gather.5.cloned.1.call-done, bf16[512,5120]{0,1:T(8,128)(2,1)} %gather.7, pred[5120]{0:T(1024)(128)(4,1)S(1)} %broadcast_in_dim.101, f32[256]{0:T(256)S(1)} %dynamic-slice_convert_fusion), kind=kOutput, calls=%fused_computation.43 | convolution fusion | flops 1344929792 | bytes 8394752 | tf_op jit(solution)/shard_map/dot_general | solution.py:98
  127.8 4.6 %all-gather.7.cloned.1.call-done = bf16[8192,256]{0,1:T(8,128)(2,1)} async-done(((bf16[512,256]{0,1:T(8,128)(2,1)}), bf16[8192,256]{0,1:T(8,128)(2,1)}) %all-gather.7.cloned.1.call-update) | async-done | bytes 4194320 | tf_op jit(solution)/shard_map/all_gather | solution.py:31
  132.4 4.6 %fusion.44 = (bf16[8192,128]{0,1:T(8,128)(2,1)}, bf16[8192,128]{0,1:T(8,128)(2,1)}) fusion(bf16[8192,256]{0,1:T(8,128)(2,1)} %all-gather.7.cloned.1.call-done), kind=kLoop, calls=%fused_computation.75 | loop fusion | bytes 8388608 | tf_op jit(solution)/shard_map/slice | solution.py:33
  137.1 71.6 %while.18 = (s32[]{:T(128)}, f32[2,512]{1,0:T(2,128)S(1)}, f32[2,512]{1,0:T(2,128)S(1)}, f32[2,512,128]{2,1,0:T(8,128)S(1)}, s32[8192]{0:T(1024)S(1)}, /*index=5...) while((s32[]{:T(128)}, f32[2,512]{1,0:T(2,128)S(1)}, ...), condition=%wide.region_4.5_spmd.clone, body=%wide.region_1.4_spmd.clone.sunk | while | flops 276436992 | bytes 8995027 | solution.py:158
  157.4 2.0 convolution_add_fusion.2
  208.9 5.6 %convolution_convert_fusion = bf16[512,5120]{1,0:T(8,128)(2,1)} fusion(bf16[512,256]{0,1:T(8,128)(2,1)S(1)} %bitcast.74, bf16[256,5120]{0,1:T(8,128)(2,1)} %all-gather.9.cloned.1.call-done), kind=kOutput, calls=%fused_computation.36 | convolution fusion | flops 1344798720 | bytes 8126464 | tf_op jit(solution)/shard_map/dot_general | solution.py:167
  214.6 59.1 %reduce-scatter.5.cloned.1.call-done = bf16[512,1280]{1,0:T(8,128)(2,1)} async-done(((bf16[512,5120]{1,0:T(8,128)(2,1)}), bf16[512,1280]{1,0:T(8,128)(2,1)}) %reduce-scatter.5.cloned.1.call-update) | async-done | bytes 1310736 | tf_op jit(solution)/shard_map/reduce_scatter | solution.py:41
  273.7 2.4 copy.49
  276.2 37.3 %reduce-scatter.7.cloned.1.call-done = bf16[320,512]{1,0:T(8,128)(2,1)} async-done(((bf16[1280,512]{1,0:T(8,128)(2,1)}), bf16[320,512]{1,0:T(8,128)(2,1)}) %reduce-scatter.7.cloned.1.call-update) | async-done | bytes 327696
  (212 shorter events, 83.1 us)
Async XLA Ops:
  6.5 39.4 %copy-start.3 = (bf16[5120]{0:T(1024)(128)(2,1)S(1)}, bf16[5120]{0:T(1024)(128)(2,1)}, u32[]{:S(2)}) copy-start(bf16[5120]{0:T(1024)(128)(2,1)} %param.13) | copy-start | bytes 30724
  8.1 21.6 %all-to-all-start.1 = ((bf16[20,16,128]{2,0,1:T(8,128)(2,1)}), bf16[20,16,128]{2,0,1:T(8,128)(2,1)S(1)}, u32[]{:S(2)}, u32[]{:S(2)}) async-start(bf16[20,16,128]{2,0,1:T(8,128)(2,1)} %copy.37), calls=%async_computation.1 | async-start | bytes 196608 | tf_op jit(solution)/shard_map/all_to_all | solution.py:93
  29.8 15.3 %all-to-all-start = ((bf16[20,16,256]{2,0,1:T(8,128)(2,1)}), bf16[20,16,256]{2,0,1:T(8,128)(2,1)S(1)}, u32[]{:S(2)}, u32[]{:S(2)}) async-start(bf16[20,16,256]{2,0,1:T(8,128)(2,1)} %copy.36), calls=%async_computation | async-start | bytes 393216 | tf_op jit(solution)/shard_map/all_to_all | solution.py:92
  33.3 54.7 %all-gather.5.cloned.1.call-start = ((), (), s32[]{:S(2)}) async-start(), calls=%async_computation.5 | async-start | bytes 5570560 | tf_op jit(solution)/shard_map/all_gather | solution.py:31
  33.4 9.4 %collective-permute-start = (bf16[320,128]{1,0:T(8,128)(2,1)S(1)}, bf16[320,128]{1,0:T(8,128)(2,1)S(1)}, u32[]{:S(2)}, u32[]{:S(2)}) collective-permute-start(bf16[320,128]{1,0:T(8,128)(2,1)S(1)} %all_to_all.49), channel_id=1, source_target_pairs={{0,1},{1,0},{2,3},{3,2},{4,5},{5,4},{6,7},{7,6},{8,9},{9,8},{10,11... | collective-permute-start | bytes 245768 | tf_op jit(solution)/shard_map/ppermute | solution.py:26
  45.9 86.6 %all-gather.7.cloned.1.call-start = ((), (), s32[]{:S(2)}) async-start(), calls=%async_computation.6 | async-start | bytes 4456448 | tf_op jit(solution)/shard_map/all_gather | solution.py:31
  45.9 4.0 %copy-start = (bf16[512,5120]{1,0:T(8,128)(2,1)S(1)}, bf16[512,5120]{1,0:T(8,128)(2,1)}, u32[]{:S(2)}) copy-start(bf16[512,5120]{1,0:T(8,128)(2,1)} %param.12) | copy-start | bytes 15728644
  62.4 9.0 %copy-start.5 = (s32[256]{0:T(256)S(1)}, s32[256]{0:T(256)}, u32[]{:S(2)}) copy-start(s32[256]{0:T(256)} %param.19) | copy-start | bytes 3076
  77.8 9.3 %copy-start.4 = (s32[512]{0:T(512)S(1)}, s32[512]{0:T(512)}, u32[]{:S(2)}) copy-start(s32[512]{0:T(512)} %param.20) | copy-start | bytes 6148
  93.7 1.9 copy-start.1
  93.7 8.0 %copy-start.2 = (s32[512]{0:T(512)S(1)}, s32[512]{0:T(512)}, u32[]{:S(2)}) copy-start(s32[512]{0:T(512)} %param.21) | copy-start | bytes 6148
  96.4 23.8 %all-to-all-start.2 = ((bf16[16,256,20]{1,2,0:T(8,128)(2,1)}), bf16[16,256,20]{1,2,0:T(8,128)(2,1)S(1)}, u32[]{:S(2)}, u32[]{:S(2)}) async-start(bf16[16,256,20]{1,2,0:T(8,128)(2,1)} %copy.46), calls=%async_computation.2 | async-start | bytes 393216 | tf_op jit(solution)/shard_map/all_to_all | solution.py:166
  101.6 107.3 %all-gather.9.cloned.1.call-start = ((), (), s32[]{:S(2)}) async-start(), calls=%async_computation.7 | async-start | bytes 2785280 | tf_op jit(solution)/shard_map/all_gather | solution.py:169
  120.9 152.8 %reduce-scatter.5.cloned.1.call-start = ((), (), s32[]{:S(2)}) async-start(), calls=%async_computation.8 | async-start | bytes 6553600 | tf_op jit(solution)/shard_map/reduce_scatter | solution.py:41
  214.6 98.9 %reduce-scatter.7.cloned.1.call-start = ((), (), s32[]{:S(2)}) async-start(), calls=%async_computation.9 | async-start | bytes 1638400
Sparse Core Ops, SparseCore 0:
  46.0 37.4 all-gather.4
  95.7 36.7 all-gather.6
  134.3 37.1 all-gather.8
  214.7 58.9 reduce-scatter.4
  276.3 37.1 reduce-scatter.6
where the time goes:
time: 326 us; the launch traced here: 323 us
  waiting for transfers between devices  119 us (37%)
  matrix products  72.4 us (22%)
  local copies, waits for them, and re-layouts  48.9 us (15%)
  other arithmetic  28 us (9%)
  starting transfers between devices  23.2 us (7%)
  blocking collectives  17.7 us (5%)
  between operations  13.5 us (4%)
    reduce_scatter x1, waiting for transfers between devices, sum_by_axis(): nearer = lax.psum_scatter(x, axes[0], scatter_dimension=dim, tiled=True)  59.1 us
    unnamed x6, waiting for transfers between devices  37.4 us
    dot_general x16, matrix products, one_block(): jnp.einsum('hqk,kd->hqd', raw_weights.astype(jnp.bfloat16), value_block,...  31.5 us
    dot_general x16, matrix products, one_block(): jnp.einsum('qhd,kd->hqk', query_rot, key_block, preferred_element_type=jn...  23.8 us
    all_gather x1, blocking collectives, per_device(): lax.all_gather(segments, 'blk', axis=0, tiled=True)  17.7 us
    gather x2, local copies, waits for them, and re-layouts, per_device(): jnp.take(normed.reshape(local_tokens, device_map.shape[0], shard_rows), d...  15.4 us
    all_to_all x1, starting transfers between devices, per_device(): lax.all_to_all(w_key_value, TP, split_axis=1, concat_axis=0, tiled=True)  11.2 us
    reduce_sum x16, other arithmetic, one_block(): run_mass = run_mass * factor + jnp.sum(raw_weights, axis=2)  9.08 us
  transfers between devices with their start and end apart: 9, of which 6 were waited for; matrix products, arithmetic and copies ran while one was open for 39% of the time, Pallas kernels for 0%

commit v1 on v0

v1 whole, which is shorter than its diff:
```python
import functools

import jax
import jax.numpy as jnp
from jax import lax
from jax.experimental import pallas as pl
from jax.experimental.pallas import tpu as pltpu
from jax.sharding import PartitionSpec as P

D = 5120
HD = 128
TOK = 512
ROWS = 20
NORM_FLOOR = 0.0625
ROPE_BASE = 1000000.0
NEGATIVE_FILL = -1e30
LOG2E = 1.4426950408889634
MESH = pl.DeviceIdType.MESH
VM = pltpu.VMEM
BF = jnp.bfloat16
F32 = jnp.float32
VLIM = 62 * 1024 * 1024


def coords():
    b = lax.axis_index("blk")
    t = lax.axis_index("tp")
    x = b // 4
    zl = (b // 2) % 2
    c = b % 2
    y = t // 4
    zh = t % 4
    return b, t, x, zl, c, y, zh


def blk_of(x, zl, c):
    return x * 4 + zl * 2 + c


def signal(dev):
    pl.semaphore_signal(pltpu.get_barrier_semaphore(), inc=1, device_id=dev, device_id_type=MESH)


def push(src, dst, ssem, rsem, dev):
    pltpu.make_async_remote_copy(src, dst, ssem, rsem, device_id=dev, device_id_type=MESH).start()


class Gather:
    def __init__(self, at, pieces, send, recv):
        self.at, self.n, self.send, self.recv = at, pieces, send, recv
        b, t, x, zl, c, y, zh = coords()
        self.t = t
        self.own = b
        self.sib = blk_of(x, zl, 1 - c)
        self.z = blk_of(x, 1 - zl, c)
        xp, xm, x2 = (x + 1) % 4, (x + 3) % 4, (x + 2) % 4
        self.xp, self.xm = blk_of(xp, zl, c), blk_of(xm, zl, c)
        self.xpz, self.xmz = blk_of(xp, 1 - zl, c), blk_of(xm, 1 - zl, c)
        self.x2, self.x2z = blk_of(x2, zl, c), blk_of(x2, 1 - zl, c)
        self.count = 0
        self.sent = []

    def peers(self):
        return [self.sib, self.z, self.xp, self.xm]

    def _send(self, chunk, p, to):
        ref = self.at(chunk, p)
        k = self.count
        self.count += 1
        push(ref, ref, self.send.at[k], self.recv.at[chunk, p], {"blk": to, "tp": self.t})
        self.sent.append((chunk, p, k))

    def wait(self, chunk, p):
        ref = self.at(chunk, p)
        pltpu.make_async_copy(ref, ref, self.recv.at[chunk, p]).wait()

    def own_piece(self, p):
        for to in (self.xp, self.xm, self.z, self.sib):
            self._send(self.own, p, to)

    def z_piece(self, p):
        self.wait(self.z, p)
        for to in (self.xp, self.xm, self.sib):
            self._send(self.z, p, to)

    def side(self, p, zside):
        minus, plus = (self.xmz, self.xpz) if zside else (self.xm, self.xp)
        half = self.n // 2
        self.wait(minus, p)
        if p < half:
            self._send(minus, p, self.xp)
        self._send(minus, p, self.sib)
        self.wait(plus, p)
        if p >= half:
            self._send(plus, p, self.xm)
        self._send(plus, p, self.sib)

    def far(self, p, zside):
        chunk = self.x2z if zside else self.x2
        self.wait(chunk, p)
        self._send(chunk, p, self.sib)

    def forward_all(self):
        for p in range(self.n):
            self.z_piece(p)
        for zside in (False, True):
            for p in range(self.n):
                self.side(p, zside)
        for zside in (False, True):
            for p in range(self.n):
                self.far(p, zside)

    def sibling_chunks(self):
        flip = lambda k: k + 1 - 2 * (k % 2)
        return [flip(k) for k in (self.own, self.z, self.xm, self.xp, self.xmz, self.xpz, self.x2, self.x2z)]

    def wait_sibling(self):
        for chunk in self.sibling_chunks():
            for p in range(self.n):
                self.wait(chunk, p)

    def drain(self):
        for chunk, p, k in self.sent:
            ref = self.at(chunk, p)
            pltpu.make_async_copy(ref, ref, self.send.at[k]).wait()


def sends_of(pieces):
    return 15 * pieces


def prep_kernel(dm, x_ref, gain_ref, out_ref, slot, five):
    acc = jnp.zeros((TOK, 128), F32)
    for j in range(D // 128):
        v = x_ref[:, j * 128 : (j + 1) * 128].astype(F32)
        acc = acc + v * v
    square = jnp.maximum(jnp.sum(acc, axis=1, keepdims=True) * (1.0 / D), NORM_FLOOR)
    scale = lax.rsqrt(square)

    def turn(i, carry):
        for k in range(5):
            at = pl.ds(pl.multiple_of(i * 640 + k * 128, 128), 128)
            v = x_ref[:, at].astype(F32) * scale * gain_ref[:, at].astype(F32)
            five[k * 128 : (k + 1) * 128, :] = v.astype(BF).astype(F32).T
        for k in range(32):
            slot[i * 32 + k] = five[k * ROWS : (k + 1) * ROWS, :]
        return carry

    lax.fori_loop(0, 8, turn, 0)

    def back(i, carry):
        for k in range(32):
            five[k * ROWS : (k + 1) * ROWS, :] = slot[dm[i * 32 + k]]
        for k in range(5):
            at = pl.ds(pl.multiple_of(i * 640 + k * 128, 128), 128)
            out_ref[:, at] = five[k * 128 : (k + 1) * 128, :].T.astype(BF)
        return carry

    lax.fori_loop(0, 8, back, 0)


def prep(x, gain, device_map):
    return pl.pallas_call(
        prep_kernel,
        out_shape=jax.ShapeDtypeStruct((TOK, D), BF),
        in_specs=[pl.BlockSpec(memory_space=pltpu.SMEM), pl.BlockSpec(memory_space=VM), pl.BlockSpec(memory_space=VM)],
        out_specs=pl.BlockSpec(memory_space=VM),
        scratch_shapes=[VM((256, ROWS, TOK), F32), VM((640, TOK), F32)],
        compiler_params=pltpu.CompilerParams(vmem_limit_bytes=VLIM),
        name="prep",
    )(device_map, x, gain.reshape(1, D))


def weights_kernel(
    wq, wkv, wo, seg, ordered, bias, cos, sin, qseg,
    q_out, kv_out, wo_out, seg_out,
    land, wide, w, land_o, wide_o, wog,
    a_send, a_recv, o_send, o_recv, s_send, s_recv, g_send, g_recv, h_send, h_recv, l_sem,
):
    b, t, x, zl, c, y, zh = coords()
    main = Gather(lambda k, p: w.at[k, pl.ds(p * 80, 80)], 4, g_send, g_recv)
    outw = Gather(lambda k, p: wog.at[k, :, pl.ds(p * 512, 512)], 2, h_send, h_recv)
    tgt_blk = blk_of(x, y // 2, y % 2)
    tgt_tp = [yb * 4 + 2 * zl + c for yb in range(4)]
    src_blk = blk_of(x, zh // 2, zh % 2)
    src_tp = [(2 * zl + c) * 4 + k for k in range(4)]

    def other(kb, kt):
        return jnp.logical_or(kb != b, kt != t)

    for k in range(1, 16):
        signal({"blk": b, "tp": (t + k) % 16})
        signal({"blk": (b + k) % 16, "tp": t})
    for k in range(4):
        @pl.when(other(tgt_blk, tgt_tp[k]))
        def _():
            signal({"blk": tgt_blk, "tp": tgt_tp[k]})

        @pl.when(other(src_blk, src_tp[k]))
        def _():
            signal({"blk": src_blk, "tp": src_tp[k]})
    loop = jnp.logical_and(y == 2 * zl + c, zh == 2 * zl + c).astype(jnp.int32)
    pl.semaphore_wait(pltpu.get_barrier_semaphore(), 38 - 2 * loop)

    def q_src(to):
        return wq.at[:, pl.ds(pl.multiple_of(to * 256, 256), 256)]

    def kv_src(to):
        return wkv.at[:, pl.ds(pl.multiple_of((to // 2) * 256, 256), 256)]

    def q_land(k):
        return land.at[k, :, pl.ds(0, 256)]

    def kv_land(k):
        return land.at[k, :, pl.ds(256, 256)]

    order = [4, 12, 1, 3, 5, 7, 13, 15, 8, 2, 9, 6, 14, 10, 11]
    for k in order:
        to = (t + k) % 16
        push(q_src(to), q_land(t), a_send.at[0, k], a_recv.at[0, t], {"blk": b, "tp": to})
        push(kv_src(to), kv_land(t), a_send.at[1, k], a_recv.at[1, t], {"blk": b, "tp": to})
    pltpu.make_async_copy(q_src(t), q_land(t), a_recv.at[0, t]).start()
    pltpu.make_async_copy(kv_src(t), kv_land(t), a_recv.at[1, t]).start()
    for k in range(1, 16):
        push(seg, seg_out.at[b], s_send.at[k], s_recv.at[b], {"blk": (b + k) % 16, "tp": t})
    pltpu.make_async_copy(seg, seg_out.at[b], s_recv.at[b]).start()
    for k in range(4):
        src = wo.at[:, pl.ds(k * 1024, 1024)]

        @pl.when(other(tgt_blk, tgt_tp[k]))
        def _():
            push(src, land_o.at[zh], o_send.at[k], o_recv.at[zh], {"blk": tgt_blk, "tp": tgt_tp[k]})

        @pl.when(jnp.logical_not(other(tgt_blk, tgt_tp[k])))
        def _():
            pltpu.make_async_copy(src, land_o.at[zh], o_recv.at[zh]).start()

    for g in range(4):
        for k in range(4 * g, 4 * g + 4):
            pltpu.make_async_copy(q_src(0), q_land(k), a_recv.at[0, k]).wait()
            pltpu.make_async_copy(kv_src(0), kv_land(k), a_recv.at[1, k]).wait()
            wide[pl.ds(k * ROWS, ROWS), :] = land[k].astype(F32)
        w[b, pl.ds(g * 80, 80), :] = wide[pl.ds(g * 80, 80), :].astype(BF)
        main.own_piece(g)
    main.forward_all()
    for k in range(4):
        pltpu.make_async_copy(wo.at[:, pl.ds(0, 1024)], land_o.at[k], o_recv.at[k]).wait()
        wide_o[pl.ds(k * ROWS, ROWS), :] = land_o[k].astype(F32)
    wog[b] = wide_o[...].astype(BF)
    for p in range(2):
        outw.own_piece(p)
    main.wait_sibling()

    half = TOK // 2
    for r in range(2):
        rows = pl.ds(r * half, half)
        v = jnp.dot(ordered[rows, :], w[...].reshape(D, 512), preferred_element_type=F32) + bias[...]
        cs, sn = cos[rows, :], sin[rows, :]
        for h in range(3):
            u = v[:, h * HD : (h + 1) * HD]
            rot = u * cs + pltpu.roll(u, HD // 2, 1) * sn
            if h < 2:
                q_out[h, rows, 0:HD] = rot.astype(BF)
                q_out[h, rows, HD : 2 * HD] = qseg[rows, :]
            else:
                kv_out[rows, 0:HD] = rot.astype(BF)
        kv_out[rows, HD : 2 * HD] = v[:, 3 * HD :].astype(BF)
    outw.forward_all()
    outw.wait_sibling()
    wo_out[...] = wog[...]
    for k in range(16):
        pltpu.make_async_copy(seg, seg_out.at[k], s_recv.at[k]).wait()
    for k in range(1, 16):
        pltpu.make_async_copy(q_src(0), q_land(0), a_send.at[0, k]).wait()
        pltpu.make_async_copy(kv_src(0), kv_land(0), a_send.at[1, k]).wait()
        pltpu.make_async_copy(seg, seg_out.at[0], s_send.at[k]).wait()
    for k in range(4):
        @pl.when(other(tgt_blk, tgt_tp[k]))
        def _():
            pltpu.make_async_copy(wo.at[:, pl.ds(0, 1024)], land_o.at[k], o_send.at[k]).wait()
    main.drain()
    outw.drain()


def weights(wq, wkv, wo, seg, ordered, bias, cos, sin, qseg):
    hbm = pl.BlockSpec(memory_space=pl.ANY)
    vm = pl.BlockSpec(memory_space=VM)
    dma = pltpu.SemaphoreType.DMA
    return pl.pallas_call(
        weights_kernel,
        out_shape=(
            jax.ShapeDtypeStruct((2, TOK, 256), BF),
            jax.ShapeDtypeStruct((TOK, 256), BF),
            jax.ShapeDtypeStruct((16, 80, 1024), BF),
            jax.ShapeDtypeStruct((16, 1, TOK), jnp.int32),
        ),
        in_specs=[hbm, hbm, hbm, vm, vm, vm, vm, vm, vm],
        out_specs=(vm, vm, vm, vm),
        scratch_shapes=[
            VM((16, ROWS, 512), BF),
            VM((320, 512), F32),
            VM((16, 320, 512), BF),
            VM((4, ROWS, 1024), BF),
            VM((80, 1024), F32),
            VM((16, 80, 1024), BF),
            dma((2, 16)), dma((2, 16)), dma((4,)), dma((4,)), dma((16,)), dma((16,)),
            dma((sends_of(4),)), dma((16, 4)), dma((sends_of(2),)), dma((16, 2)), dma((2,)),
        ],
        compiler_params=pltpu.CompilerParams(collective_id=0, has_side_effects=True, vmem_limit_bytes=VLIM),
        name="weights",
    )(wq, wkv, wo, seg, ordered, bias, cos, sin, qseg)


def attend_kernel(q, kv, kaug, ctx, kvg, m_s, acc_s, g_send, g_recv):
    b, t, x, zl, c, y, zh = coords()
    gather = Gather(lambda k, p: kvg.at[k, pl.ds(p * 128, 128)], 4, g_send, g_recv)
    peers = gather.peers()
    for k in peers:
        signal({"blk": k, "tp": t})
    pl.semaphore_wait(pltpu.get_barrier_semaphore(), 4)
    kvg[b] = kv[...]
    for p in range(4):
        gather.own_piece(p)
    coef = HD ** -0.5 * LOG2E
    half = TOK // 2

    def block(j, diagonal):
        kop = jnp.concatenate([kvg[j, :, 0:HD], kaug[j]], axis=1)
        vop = jnp.concatenate([kvg[j, :, HD:], jnp.ones((TOK, HD), BF)], axis=1)
        for h in range(2):
            for r in range(2):
                rows = pl.ds(r * half, half)
                s = lax.dot_general(q[h, rows, :], kop, (((1,), (1,)), ((), ())), preferred_element_type=F32)
                if diagonal:
                    qi = lax.broadcasted_iota(jnp.int32, s.shape, 0) + r * half
                    ki = lax.broadcasted_iota(jnp.int32, s.shape, 1)
                    s = jnp.where(ki <= qi, s, NEGATIVE_FILL)
                peak = jnp.max(s, axis=1, keepdims=True)
                if diagonal:
                    new = peak
                else:
                    old = m_s[h, rows, :]
                    new = jnp.maximum(old, peak)
                    factor = jnp.exp2((old - new) * coef)
                e = jnp.exp2(s * coef - (new * coef)[:, 0:1]).astype(BF)
                o = jnp.dot(e, vop, preferred_element_type=F32)
                if diagonal:
                    m_s[h, rows, :] = jnp.broadcast_to(new, (half, HD))
                    acc_s[h, rows, :] = o
                else:
                    m_s[h, rows, :] = new
                    acc_s[h, rows, 0:HD] = acc_s[h, rows, 0:HD] * factor + o[:, 0:HD]
                    acc_s[h, rows, HD:] = acc_s[h, rows, HD:] * factor + o[:, HD:]

    block(b, True)
    gather.forward_all()
    gather.wait_sibling()

    def body(j, carry):
        block(j, False)
        return carry

    lax.fori_loop(0, b, body, 0)
    for h in range(2):
        ctx[:, h * HD : (h + 1) * HD] = (acc_s[h, :, 0:HD] / acc_s[h, :, HD:]).astype(BF)
    gather.drain()


def attend(q, kv, kaug):
    vm = pl.BlockSpec(memory_space=VM)
    dma = pltpu.SemaphoreType.DMA
    return pl.pallas_call(
        attend_kernel,
        out_shape=jax.ShapeDtypeStruct((TOK, 256), BF),
        in_specs=[vm, vm, vm],
        out_specs=vm,
        scratch_shapes=[
            VM((16, TOK, 256), BF),
            VM((2, TOK, HD), F32),
            VM((2, TOK, 2 * HD), F32),
            dma((sends_of(4),)), dma((16, 4)),
        ],
        compiler_params=pltpu.CompilerParams(collective_id=1, has_side_effects=True, vmem_limit_bytes=VLIM),
        name="attend",
    )(q, kv, kaug)


def out_kernel(ctx, wo, res, out, cg, far, plus, minus, r_far, r_plus, r_minus, c_send, c_recv, p_send, p_recv):
    b, t, x, zl, c, y, zh = coords()
    up, down, opp = (zh + 1) % 4, (zh + 3) % 4, (zh + 2) % 4
    yp, ym, y2 = (y + 1) % 4, (y + 3) % 4, (y + 2) % 4
    zdev = lambda k: {"blk": b, "tp": y * 4 + k}
    ydev = lambda k: {"blk": b, "tp": k * 4 + zh}
    for dev in (zdev(up), zdev(down), ydev(yp), ydev(ym)):
        signal(dev)
    pl.semaphore_wait(pltpu.get_barrier_semaphore(), 4)
    cg[zh] = ctx[...]
    at = lambda k, p: cg.at[k, pl.ds(p * 256, 256)]

    def waitc(k, p):
        pltpu.make_async_copy(at(k, p), at(k, p), c_recv.at[k, p]).wait()

    for p in range(2):
        push(at(zh, p), at(zh, p), c_send.at[p], c_recv.at[zh, p], zdev(up))
        push(at(zh, 1 - p), at(zh, 1 - p), c_send.at[2 + p], c_recv.at[zh, 1 - p], zdev(down))
    waitc(down, 0)
    push(at(down, 0), at(down, 0), c_send.at[4], c_recv.at[down, 0], zdev(up))
    waitc(up, 1)
    push(at(up, 1), at(up, 1), c_send.at[5], c_recv.at[up, 1], zdev(down))
    waitc(down, 1)
    waitc(up, 0)
    waitc(opp, 0)
    waitc(opp, 1)

    def partial(k):
        rows = pl.ds(pl.multiple_of(k * 320, 64), 320)
        v = jnp.zeros((320, TOK), F32)
        for i in range(4):
            v = v + lax.dot_general(
                wo[rows, i * 256 : (i + 1) * 256], cg[i], (((1,), (1,)), ((), ())), preferred_element_type=F32
            )
        return v

    far[...] = partial(y2).astype(BF)
    lo, hi = pl.ds(0, 160), pl.ds(160, 160)
    push(far.at[lo], r_far.at[lo], p_send.at[0], p_recv.at[0], ydev(yp))
    push(far.at[hi], r_far.at[hi], p_send.at[1], p_recv.at[1], ydev(ym))
    v = partial(yp)
    plus[hi, :] = v[160:].astype(BF)
    push(plus.at[hi], r_plus.at[hi], p_send.at[2], p_recv.at[2], ydev(yp))
    u = partial(ym)
    minus[lo, :] = u[:160].astype(BF)
    push(minus.at[lo], r_minus.at[lo], p_send.at[3], p_recv.at[3], ydev(ym))
    pltpu.make_async_copy(far.at[lo], r_far.at[lo], p_recv.at[0]).wait()
    plus[lo, :] = (v[:160] + r_far[lo, :].astype(F32)).astype(BF)
    push(plus.at[lo], r_plus.at[lo], p_send.at[4], p_recv.at[4], ydev(yp))
    pltpu.make_async_copy(far.at[hi], r_far.at[hi], p_recv.at[1]).wait()
    minus[hi, :] = (u[160:] + r_far[hi, :].astype(F32)).astype(BF)
    push(minus.at[hi], r_minus.at[hi], p_send.at[5], p_recv.at[5], ydev(ym))
    mine = partial(y) + res[...].astype(F32)
    for half, k1, k2 in ((hi, 2, 5), (lo, 4, 3)):
        pltpu.make_async_copy(plus.at[half], r_plus.at[half], p_recv.at[k1]).wait()
        pltpu.make_async_copy(minus.at[half], r_minus.at[half], p_recv.at[k2]).wait()
    out[...] = (mine + r_plus[...].astype(F32) + r_minus[...].astype(F32)).astype(BF)
    for k in range(6):
        pltpu.make_async_copy(at(0, 0), at(0, 0), c_send.at[k]).wait()
        pltpu.make_async_copy(far.at[lo], r_far.at[lo], p_send.at[k]).wait()


def project(ctx, wo, res):
    vm = pl.BlockSpec(memory_space=VM)
    dma = pltpu.SemaphoreType.DMA
    return pl.pallas_call(
        out_kernel,
        out_shape=jax.ShapeDtypeStruct((320, TOK), BF),
        in_specs=[vm, vm, vm],
        out_specs=vm,
        scratch_shapes=[VM((4, TOK, 256), BF)] + [VM((320, TOK), BF)] * 6
        + [dma((6,)), dma((4, 2)), dma((6,)), dma((6,))],
        compiler_params=pltpu.CompilerParams(collective_id=2, has_side_effects=True, vmem_limit_bytes=VLIM),
        name="project",
    )(ctx, wo, res)


def per_device(residual_in, norm_gain, w_query, w_key_value, query_bias, key_value_bias, w_output, device_map, positions, segments):
    t = lax.axis_index("tp")
    ordered = prep(residual_in, norm_gain, device_map)
    frequency = ROPE_BASE ** (-(jnp.arange(HD // 2, dtype=F32) * 2.0) / HD)
    angles = positions.astype(F32)[:, None] * frequency[None, :]
    cos, sin = jnp.cos(angles), jnp.sin(angles)
    cos = jnp.concatenate([cos, cos], axis=1)
    sin = jnp.concatenate([-sin, sin], axis=1)
    bias = jnp.concatenate(
        [
            lax.dynamic_slice_in_dim(query_bias, t * 256, 256),
            lax.dynamic_slice_in_dim(key_value_bias, (t // 2) * 256, 256),
        ]
    ).astype(F32)[None, :]
    lane = jnp.arange(HD, dtype=jnp.int32)[None, :] == 0
    qseg = jnp.where(lane, segments[:, None], 0).astype(BF)
    q, kv, wo, segs = weights(w_query, w_key_value, w_output.T, segments[None, :], ordered, bias, cos, sin, qseg)
    kaug = jnp.where(lane[None], jnp.where(segs.reshape(16, TOK, 1) == 0, NEGATIVE_FILL, 0.0), 0.0).astype(BF)
    ctx = attend(q, kv, kaug)
    res = lax.dynamic_slice_in_dim(residual_in, t * 320, 320, 1).T
    return project(ctx, wo.reshape(1280, 1024), res).T


def solution(mesh):
    both = ("blk", "tp")
    placed = (P("blk", None), P(), P(both, None), P(both, None), P(), P(), P(None, both), P(), P("blk"), P("blk"))
    return jax.shard_map(per_device, mesh=mesh, in_specs=placed, out_specs=P("blk", "tp"), check_vma=False)
```

time: 326 us -> 174 us (0.53)
  the two profiles are of different devices: /device:TPU:6 before, /device:TPU:38 now
where the time goes in v1:
time: 174 us
  Pallas kernels  159 us (91%)
  other arithmetic  7.83 us (4%)
  local copies, waits for them, and re-layouts  6.71 us (4%)
    pallas_call x1, Pallas kernels, weights(): pl.pallas_call(weights_kernel, out_shape=(jax.ShapeDtypeStruct((2, TOK, 2...  64.4 us
    pallas_call x1, Pallas kernels, attend(): pl.pallas_call(attend_kernel, out_shape=jax.ShapeDtypeStruct((TOK, 256),...  45.9 us
    pallas_call x1, Pallas kernels, project(): pl.pallas_call(out_kernel, out_shape=jax.ShapeDtypeStruct((320, TOK), BF)...  38.3 us
    pallas_call x1, Pallas kernels, prep(): pl.pallas_call(prep_kernel, out_shape=jax.ShapeDtypeStruct((TOK, D), BF),...  10.8 us

profile of v1, /device:TPU:38, one launch (start us, length us, event | category | flops | bytes accessed | tf_op | source)
XLA Modules:
  0.0 174.0 jit_solution(9683813682387000800)
XLA Ops:
  0.0 0.8 dynamic_slice.10
  0.8 0.8 dynamic_slice.9
  1.5 0.6 maximum_convert_fusion.bias
  2.1 0.7 convert_element_type.20
  2.8 1.0 fusion
  3.8 1.0 pad_maximum_fusion
  4.8 1.5 select_convert_fusion.1.qseg
  6.3 1.3 reshape.68.gain_ref
  7.6 10.8 %prep.1.ordered = bf16[512,5120]{1,0:T(8,128)(2,1)} custom-call(s32[256]{0:T(256)} %dm.1, bf16[512,5120]{1,0:T(8,128)(2,1)} %x_ref.1, bf16[1,5120]{1,0:T(2,128)(2,1)} %reshape.68.gain_ref), custom_call_target="tpu_custom_call" | custom-call | tf_op jit(solution)/shard_map/prep/pallas_call | solution.py:163
  18.4 64.4 %weights.1 = (bf16[2,512,256]{2,1,0:T(8,128)(2,1)}, bf16[512,256]{1,0:T(8,128)(2,1)}, bf16[16,80,1024]{2,1,0:T(8,128)(2,1)}, s32[16,1,512]{2,1,0:T(1,128)}) custom-call(bf16[20,4096]{1,0:T(8,128)(2,1)} %wq.1, bf16[20,2048]{1,0:T(8,128)(2,1)} %wkv.1, bf16[20,4096]{1,0:T(8,128)(2,1)} %bitcast.11, s32[1,512]{1,0:T(1,128)} %bitcast.13, ...), custom_call_target="tpu_custom_call" | custom-call | tf_op jit(solution)/shard_map/weights/pallas_call | solution.py:289
  82.8 0.8 compare_select_fusion
  83.6 2.3 %select_convert_fusion.kaug = bf16[16,512,128]{2,1,0:T(8,128)(2,1)} fusion(bf16[16,512]{1,0:T(8,128)(2,1)S(1)} %bitcast.12, pred[128]{0:T(512)(128)(4,1)S(1)} %iota_compare_fusion), kind=kLoop, calls=%fused_computation | loop fusion | flops 1048576 | bytes 2113664 | tf_op jit(solution)/shard_map/convert_element_type | solution.py:482
  85.9 45.9 %attend.1.ctx = bf16[512,256]{1,0:T(8,128)(2,1)} custom-call(bf16[2,512,256]{2,1,0:T(8,128)(2,1)} %get-tuple-element.9.q, bf16[512,256]{1,0:T(8,128)(2,1)} %get-tuple-element.10.kv, bf16[16,512,128]{2,1,0:T(8,128)(2,1)} %select_convert_fusion.kaug), custom_call_target="tpu_custom_call" | custom-call | tf_op jit(solution)/shard_map/attend/pallas_call | solution.py:372
  131.8 1.2 constant_dynamic-slice_fusion
  133.1 0.9 copy.13
  134.0 38.3 %project.1 = bf16[320,512]{1,0:T(8,128)(2,1)} custom-call(bf16[512,256]{1,0:T(8,128)(2,1)} %attend.1.ctx, bf16[1280,1024]{1,0:T(8,128)(2,1)} %bitcast.8, bf16[320,512]{1,0:T(8,128)(2,1)} %bitcast.9), custom_call_target="tpu_custom_call" | custom-call | tf_op jit(solution)/shard_map/project/pallas_call | solution.py:453
  172.3 1.7 copy.17
  (5 shorter events, 0.0 us)

commit v2 on v0

v2 whole, which is shorter than its diff:
```python
import jax
import jax.numpy as jnp
import numpy as np
from jax import lax
from jax.experimental import pallas as pl
from jax.experimental.pallas import tpu as pltpu
from jax.sharding import PartitionSpec as P

D = 5120
HD = 128
TOK = 512
ROWS = 20
WC = 384
NORM_FLOOR = 0.0625
ROPE_BASE = 1000000.0
NEGATIVE_FILL = -1e30
LOG2E = 1.4426950408889634
MESH = pl.DeviceIdType.MESH
VM = pltpu.VMEM
DMA = pltpu.SemaphoreType.DMA
BF = jnp.bfloat16
F32 = jnp.float32
VLIM = 62 * 1024 * 1024
PIO2 = (1.5703125, 4.83751296997e-04, 7.54978995489e-08)


def coords():
    b = lax.axis_index("blk")
    t = lax.axis_index("tp")
    return b, t, b // 4, (b // 2) % 2, b % 2, t // 4, t % 4


def blk_of(x, zl, c):
    return x * 4 + zl * 2 + c


def signal(dev):
    pl.semaphore_signal(pltpu.get_barrier_semaphore(), inc=1, device_id=dev, device_id_type=MESH)


def push(src, dst, ssem, rsem, dev):
    pltpu.make_async_remote_copy(src, dst, ssem, rsem, device_id=dev, device_id_type=MESH).start()


def landed(ref, sem):
    pltpu.make_async_copy(ref, ref, sem).wait()


def sends_of(pieces):
    return 15 * pieces


class Gather:
    def __init__(self, at, pieces, send, recv):
        self.at, self.n, self.send, self.recv = at, pieces, send, recv
        b, t, x, zl, c, y, zh = coords()
        self.t = t
        self.own = b
        self.sib = blk_of(x, zl, 1 - c)
        self.z = blk_of(x, 1 - zl, c)
        xp, xm, x2 = (x + 1) % 4, (x + 3) % 4, (x + 2) % 4
        self.xp, self.xm = blk_of(xp, zl, c), blk_of(xm, zl, c)
        self.xpz, self.xmz = blk_of(xp, 1 - zl, c), blk_of(xm, 1 - zl, c)
        self.x2, self.x2z = blk_of(x2, zl, c), blk_of(x2, 1 - zl, c)
        self.order = (self.own, self.z, self.xm, self.xp, self.xmz, self.xpz, self.x2, self.x2z)
        self.count = 0
        self.sent = []

    def _send(self, chunk, p, to):
        ref = self.at(chunk, p)
        k = self.count
        self.count += 1
        push(ref, ref, self.send.at[k], self.recv.at[chunk, p], {"blk": to, "tp": self.t})
        self.sent.append((p, k))

    def wait(self, chunk, p):
        landed(self.at(chunk, p), self.recv.at[chunk, p])

    def mine(self, *pieces):
        for p in pieces:
            for to in (self.xp, self.xm, self.z, self.sib):
                self._send(self.own, p, to)

    def zfwd(self, *pieces):
        for p in pieces:
            self.wait(self.z, p)
            for to in (self.xp, self.xm, self.sib):
                self._send(self.z, p, to)

    def side(self, zside, *pieces):
        minus, plus = (self.xmz, self.xpz) if zside else (self.xm, self.xp)
        for p in pieces:
            self.wait(minus, p)
            if p % 2 == 0:
                self._send(minus, p, self.xp)
            self._send(minus, p, self.sib)
            self.wait(plus, p)
            if p % 2 == 1:
                self._send(plus, p, self.xm)
            self._send(plus, p, self.sib)

    def far(self, zside, *pieces):
        chunk = self.x2z if zside else self.x2
        for p in pieces:
            self.wait(chunk, p)
            self._send(chunk, p, self.sib)

    def sibs(self, k):
        chunk = flip(self.order[k])
        for p in range(self.n):
            self.wait(chunk, p)

    def drain(self):
        for p, k in self.sent:
            landed(self.at(0, p), self.send.at[k])


def flip(k):
    return k + 1 - 2 * (k % 2)


def pick(options, i):
    r = options[0]
    for k in range(1, len(options)):
        r = jnp.where(i == k, options[k], r)
    return r


def run(n, compute, events):
    def body(i, carry):
        for k, event in events.items():
            pl.when(i == k)(event)
        compute(i)
        return carry

    lax.fori_loop(0, n, body, 0)


def seq(*calls):
    def go():
        for f, *args in calls:
            f(*args)

    return go


def cos_sin(angle):
    k = jnp.floor(angle * (2.0 / np.pi) + 0.5)
    r = ((angle - k * PIO2[0]) - k * PIO2[1]) - k * PIO2[2]
    s = r * r
    sin = r + r * s * (-1.6666654611e-1 + s * (8.3321608736e-3 + s * -1.9515295891e-4))
    cos = 1.0 - 0.5 * s + s * s * (4.166664568298827e-2 + s * (-1.388731625493765e-3 + s * 2.443315711809948e-5))
    m = k.astype(jnp.int32)
    odd = m % 2 == 1
    cos_v = jnp.where(odd, sin, cos)
    sin_v = jnp.where(odd, cos, sin)
    cos_v = jnp.where((m + 1) // 2 % 2 == 1, -cos_v, cos_v)
    sin_v = jnp.where(m // 2 % 2 == 1, -sin_v, sin_v)
    return cos_v, sin_v


def layer(
    dm, x_hbm, wq, wkv, wo, vec, pos, seg, freq,
    out,
    xv, slot, five, ordered, land, wide, w, land_o, wide_o, wog, segs, kaug, acc_w, trig, res, q, kvg, m_s, acc_s, cg, far_b, plus, minus,
    r_far, r_plus, r_minus,
    a_send, a_recv, o_send, o_recv, s_send, s_recv, g_send, g_recv, h_send, h_recv, k_send, k_recv, e_send, c_send, c_recv, p_send, p_recv,
    x_sem,
):
    b, t, x, zl, c, y, zh = coords()
    hl = t % 2
    main = Gather(lambda k, p: w.at[k, pl.ds(p * 80, 80)], 4, g_send, g_recv)
    outw = Gather(lambda k, p: wog.at[k, :, pl.ds(p * 512, 512)], 2, h_send, h_recv)

    def kv_at(k, p):
        lane = pl.multiple_of(128 * ((hl + p // 2) % 2), 128)
        return kvg.at[k, pl.ds(256 * (p % 2), 256), pl.ds(lane, 128)]

    keys = Gather(kv_at, 4, k_send, k_recv)
    tgt_blk = blk_of(x, y // 2, y % 2)
    tgt_tp = [yb * 4 + 2 * zl + c for yb in range(4)]
    src_blk = blk_of(x, zh // 2, zh % 2)
    src_tp = [(2 * zl + c) * 4 + k for k in range(4)]

    def other(kb, kt):
        return jnp.logical_or(kb != b, kt != t)

    x_copy = pltpu.make_async_copy(x_hbm, xv, x_sem)
    x_copy.start()
    for k in range(1, 16):
        signal({"blk": b, "tp": (t + k) % 16})
        signal({"blk": (b + k) % 16, "tp": t})
    for k in range(4):
        @pl.when(other(tgt_blk, tgt_tp[k]))
        def _():
            signal({"blk": tgt_blk, "tp": tgt_tp[k]})

        @pl.when(other(src_blk, src_tp[k]))
        def _():
            signal({"blk": src_blk, "tp": src_tp[k]})
    loop = jnp.logical_and(y == 2 * zl + c, zh == 2 * zl + c).astype(jnp.int32)
    pl.semaphore_wait(pltpu.get_barrier_semaphore(), 38 - 2 * loop)

    def q_src(to):
        return wq.at[:, pl.ds(pl.multiple_of(to * 256, 256), 256)]

    def kv_src(to):
        return wkv.at[:, pl.ds(pl.multiple_of(to * 128, 128), 128)]

    def q_land(k):
        return land.at[k, :, pl.ds(0, 256)]

    def kv_land(k):
        return land.at[k, :, pl.ds(256, 128)]

    for k in (4, 12, 1, 3, 5, 7, 13, 15, 8, 2, 9, 6, 14, 10, 11):
        to = (t + k) % 16
        push(q_src(to), q_land(t), a_send.at[0, k], a_recv.at[0, t], {"blk": b, "tp": to})
        push(kv_src(to), kv_land(t), a_send.at[1, k], a_recv.at[1, t], {"blk": b, "tp": to})
    pltpu.make_async_copy(q_src(t), q_land(t), a_recv.at[0, t]).start()
    pltpu.make_async_copy(kv_src(t), kv_land(t), a_recv.at[1, t]).start()
    for k in range(1, 16):
        push(seg, segs.at[b], s_send.at[k], s_recv.at[b], {"blk": (b + k) % 16, "tp": t})
    segs[b] = seg[...]

    x_copy.wait()

    def squares(j, acc):
        v = xv[:, pl.ds(pl.multiple_of(j * 128, 128), 128)].astype(F32)
        return acc + v * v

    total = lax.fori_loop(0, D // 128, squares, jnp.zeros((TOK, 128), F32))
    square = jnp.maximum(jnp.sum(total, axis=1, keepdims=True) * (1.0 / D), NORM_FLOOR)
    trig[0] = jnp.broadcast_to(lax.rsqrt(square), (TOK, 128))

    def turn(i, carry):
        for k in range(5):
            at = pl.ds(pl.multiple_of(i * 640 + k * 128, 128), 128)
            v = xv[:, at].astype(F32) * trig[0] * vec[:, at]
            five[k * 128 : (k + 1) * 128, :] = v.astype(BF).astype(F32).T
        for k in range(32):
            slot[i * 32 + k] = five[k * ROWS : (k + 1) * ROWS, :]
        return carry

    lax.fori_loop(0, 8, turn, 0)

    def back(i):
        for k in range(32):
            five[k * ROWS : (k + 1) * ROWS, :] = slot[dm[i * 32 + k]]
        for k in range(5):
            at = pl.ds(pl.multiple_of(i * 640 + k * 128, 128), 128)
            ordered[:, at] = five[k * 128 : (k + 1) * 128, :].T.astype(BF)

    def group(g):
        for k in range(4):
            landed(q_land(4 * g + k), a_recv.at[0, 4 * g + k])
            landed(kv_land(4 * g + k), a_recv.at[1, 4 * g + k])
            wide[k * ROWS : (k + 1) * ROWS, :] = land[4 * g + k].astype(F32)
        w[b, pl.ds(g * 80, 80), :] = wide[...].astype(BF)
        main.mine(g)

    def send_out():
        for k in range(4):
            src = wo.at[:, pl.ds(k * 1024, 1024)]

            @pl.when(other(tgt_blk, tgt_tp[k]))
            def _():
                push(src, land_o.at[zh], o_send.at[k], o_recv.at[zh], {"blk": tgt_blk, "tp": tgt_tp[k]})

            @pl.when(jnp.logical_not(other(tgt_blk, tgt_tp[k])))
            def _():
                pltpu.make_async_copy(src, land_o.at[zh], o_recv.at[zh]).start()

    run(8, back, {
        0: seq((group, 0)),
        1: seq((group, 1)),
        2: seq((group, 2), (main.zfwd, 0)),
        3: seq((group, 3), (main.zfwd, 1)),
        4: seq((send_out,), (main.zfwd, 2), (main.side, False, 0)),
        5: seq((main.zfwd, 3), (main.side, False, 1)),
        6: seq((main.side, False, 2)),
        7: seq((main.side, False, 3)),
    })

    angle = freq[...] * pos[...].astype(F32)
    cos_t, sin_t = cos_sin(angle)
    trig[0] = jnp.concatenate([cos_t, cos_t], axis=0).T
    trig[1] = jnp.concatenate([-sin_t, sin_t], axis=0).T
    window = pl.ds(pl.multiple_of(128 * ((5 * t) // 2), 128), 384)
    res[...] = xv[:, window].astype(F32).T

    acc_w[...] = jnp.zeros((TOK, WC), F32)
    row0 = lax.broadcasted_iota(jnp.int32, (HD, TOK), 0) == 0

    def mul(i):
        pair = pick(main.order, i) // 2
        lanes = pl.ds(pl.multiple_of(pair * 640, 640), 640)
        acc_w[...] += jnp.dot(
            ordered[:, lanes], w[pl.ds(pair * 2, 2)].reshape(640, WC), preferred_element_type=F32
        )
        for k in range(2):
            j = 2 * i + k

            @pl.when(j != b)
            def _():
                landed(segs.at[j], s_recv.at[j])

            row = jnp.where(segs[j] == 0, NEGATIVE_FILL, 0.0)
            kaug[j] = jnp.where(row0, jnp.broadcast_to(row, (HD, TOK)), 0.0).T.astype(BF)

    run(8, mul, {
        0: seq((main.side, True, 0, 1), (main.sibs, 0)),
        1: seq((main.side, True, 2, 3), (main.sibs, 1)),
        2: seq((main.far, False, 0, 1), (main.sibs, 2)),
        3: seq((main.far, False, 2, 3), (main.sibs, 3)),
        4: seq((main.sibs, 4),),
        5: seq((main.far, True, 0, 1), (main.sibs, 5)),
        6: seq((main.far, True, 2, 3), (main.sibs, 6)),
        7: seq((main.sibs, 7),),
    })

    is_key = hl == 0
    kv_bias = vec[:, pl.ds(pl.multiple_of(D + 4096 + t * 128, 128), 128)]
    u = acc_w[:, 256:384] + kv_bias
    turned = u * trig[0] + pltpu.roll(u, HD // 2, 1) * trig[1]
    mine = pl.ds(pl.multiple_of(hl * 128, 128), 128)
    kvg[b, :, mine] = jnp.where(is_key, turned, u).astype(BF)
    partner = {"blk": b, "tp": t + 1 - 2 * hl}
    for r in range(2):
        push(kv_at(b, r), kv_at(b, r), e_send.at[r], k_recv.at[b, 2 + r], partner)
        keys.mine(r)
    own_seg = jnp.where(row0, jnp.broadcast_to(seg[...].astype(F32), (HD, TOK)), 0.0).T.astype(BF)
    for h in range(2):
        q_bias = vec[:, pl.ds(pl.multiple_of(D + t * 256 + h * 128, 128), 128)]
        u = acc_w[:, h * HD : (h + 1) * HD] + q_bias
        q[h, :, 0:HD] = (u * trig[0] + pltpu.roll(u, HD // 2, 1) * trig[1]).astype(BF)
        q[h, :, HD:] = own_seg

    coef = HD ** -0.5 * LOG2E
    half = TOK // 2

    def block(j, diagonal):
        kop = jnp.concatenate([kvg[j, :, 0:HD], kaug[j]], axis=1)
        vop = jnp.concatenate([kvg[j, :, HD:], jnp.ones((TOK, HD), BF)], axis=1)
        for h in range(2):
            for r in range(2):
                rows = pl.ds(r * half, half)
                s = lax.dot_general(q[h, rows, :], kop, (((1,), (1,)), ((), ())), preferred_element_type=F32)
                if diagonal:
                    qi = lax.broadcasted_iota(jnp.int32, s.shape, 0) + r * half
                    ki = lax.broadcasted_iota(jnp.int32, s.shape, 1)
                    s = jnp.where(ki <= qi, s, NEGATIVE_FILL)
                peak = jnp.max(s, axis=1, keepdims=True)
                if diagonal:
                    new = peak
                else:
                    old = m_s[h, rows, :]
                    new = jnp.maximum(old, peak)
                    factor = jnp.exp2((old - new) * coef)
                e = jnp.exp2(s * coef - (new * coef)[:, 0:1]).astype(BF)
                o = jnp.dot(e, vop, preferred_element_type=F32)
                if diagonal:
                    m_s[h, rows, :] = jnp.broadcast_to(new, (half, HD))
                    acc_s[h, rows, :] = o
                else:
                    m_s[h, rows, :] = new
                    acc_s[h, rows, 0:HD] = acc_s[h, rows, 0:HD] * factor + o[:, 0:HD]
                    acc_s[h, rows, HD:] = acc_s[h, rows, HD:] * factor + o[:, HD:]

    def squeeze_out():
        for k in range(4):
            landed(land_o.at[k], o_recv.at[k])
            wide_o[k * ROWS : (k + 1) * ROWS, :] = land_o[k].astype(F32)
        wog[b] = wide_o[...].astype(BF)

    keys.zfwd(0, 1)
    keys.side(False, 0, 1)
    for r in range(2):
        keys.wait(b, 2 + r)
        keys.mine(2 + r)
    squeeze_out()
    block(b, True)
    keys.zfwd(2, 3)

    def visit(i):
        chunk = pick(keys.order, i // 2)
        chunk = jnp.where(i % 2 == 1, flip(chunk), chunk)

        @pl.when(chunk < b)
        def _():
            block(chunk, False)

    run(16, visit, {
        0: seq((keys.side, False, 2, 3)),
        1: seq((keys.side, True, 0, 1), (keys.sibs, 0)),
        3: seq((keys.sibs, 1),),
        4: seq((keys.side, True, 2, 3)),
        5: seq((keys.sibs, 2),),
        6: seq((keys.far, False, 0, 1)),
        7: seq((keys.sibs, 3),),
        8: seq((outw.mine, 0, 1)),
        9: seq((keys.far, False, 2, 3), (keys.sibs, 4)),
        10: seq((keys.far, True, 0, 1)),
        11: seq((keys.sibs, 5), (outw.zfwd, 0, 1)),
        12: seq((keys.far, True, 2, 3)),
        13: seq((keys.sibs, 6), (outw.side, False, 0, 1)),
        14: seq((outw.side, True, 0, 1)),
        15: seq((keys.sibs, 7),),
    })

    up, down, opp = (zh + 1) % 4, (zh + 3) % 4, (zh + 2) % 4
    yp, ym, y2 = (y + 1) % 4, (y + 3) % 4, (y + 2) % 4
    zdev = lambda k: {"blk": b, "tp": y * 4 + k}
    ydev = lambda k: {"blk": b, "tp": k * 4 + zh}
    at = lambda k, p: cg.at[k, pl.ds(p * 128, 128)]

    def waitc(k, p):
        landed(at(k, p), c_recv.at[k, p])

    for r in range(2):
        rows = pl.ds(r * half, half)
        for h in range(2):
            cg[zh, rows, h * HD : (h + 1) * HD] = (acc_s[h, rows, 0:HD] / acc_s[h, rows, HD:]).astype(BF)
        for p in (2 * r, 2 * r + 1):
            push(at(zh, p), at(zh, p), c_send.at[0, p], c_recv.at[zh, p], zdev(up))
            push(at(zh, p), at(zh, p), c_send.at[1, p], c_recv.at[zh, p], zdev(down))
        if r == 0:
            outw.far(False, 0, 1)
        waitc(down, 2 * r)
        push(at(down, 2 * r), at(down, 2 * r), c_send.at[2, 2 * r], c_recv.at[down, 2 * r], zdev(up))
        waitc(up, 2 * r + 1)
        push(at(up, 2 * r + 1), at(up, 2 * r + 1), c_send.at[2, 2 * r + 1], c_recv.at[up, 2 * r + 1], zdev(down))
    outw.far(True, 0, 1)
    for k in range(8):
        outw.sibs(k)

    def partial(k, r):
        v = jnp.zeros((320, half), F32)
        for i in range(4):
            v = v + lax.dot_general(
                wog[pl.ds(k * 4, 4), :, i * 256 : (i + 1) * 256].reshape(320, 256),
                cg[i, pl.ds(r * half, half), :],
                (((1,), (1,)), ((), ())),
                preferred_element_type=F32,
            )
        return v

    lo, hi = pl.ds(0, 160), pl.ds(160, 160)
    for r in range(2):
        waitc(down, 2 * r + 1)
        waitc(up, 2 * r)
        waitc(opp, 2 * r)
        waitc(opp, 2 * r + 1)
        far_b[r] = partial(y2, r).astype(BF)
        push(far_b.at[r, lo], r_far.at[r, lo], p_send.at[r, 0], p_recv.at[r, 0], ydev(yp))
        push(far_b.at[r, hi], r_far.at[r, hi], p_send.at[r, 1], p_recv.at[r, 1], ydev(ym))
        v = partial(yp, r)
        plus[r, hi, :] = v[160:].astype(BF)
        push(plus.at[r, hi], r_plus.at[r, hi], p_send.at[r, 2], p_recv.at[r, 2], ydev(yp))
        u = partial(ym, r)
        minus[r, lo, :] = u[:160].astype(BF)
        push(minus.at[r, lo], r_minus.at[r, lo], p_send.at[r, 3], p_recv.at[r, 3], ydev(ym))
        landed(r_far.at[r, lo], p_recv.at[r, 0])
        plus[r, lo, :] = (v[:160] + r_far[r, lo, :].astype(F32)).astype(BF)
        push(plus.at[r, lo], r_plus.at[r, lo], p_send.at[r, 4], p_recv.at[r, 4], ydev(yp))
        landed(r_far.at[r, hi], p_recv.at[r, 1])
        minus[r, hi, :] = (u[160:] + r_far[r, hi, :].astype(F32)).astype(BF)
        push(minus.at[r, hi], r_minus.at[r, hi], p_send.at[r, 5], p_recv.at[r, 5], ydev(ym))
        cols = pl.ds(r * half, half)
        res[pl.ds(0, 320), cols] = partial(y, r) + res[pl.ds(pl.multiple_of(64 * hl, 64), 320), cols]
    for r in range(2):
        for sl, k1, k2 in ((hi, 2, 5), (lo, 4, 3)):
            landed(r_plus.at[r, sl], p_recv.at[r, k1])
            landed(r_minus.at[r, sl], p_recv.at[r, k2])
        cols = pl.ds(r * half, half)
        out[:, cols] = (res[pl.ds(0, 320), cols] + r_plus[r].astype(F32) + r_minus[r].astype(F32)).astype(BF)

    for k in range(1, 16):
        landed(q_land(0), a_send.at[0, k])
        landed(kv_land(0), a_send.at[1, k])
        landed(segs.at[0], s_send.at[k])
    for k in range(4):
        @pl.when(other(tgt_blk, tgt_tp[k]))
        def _():
            landed(land_o.at[k], o_send.at[k])

        landed(at(0, 0), c_send.at[0, k])
        landed(at(0, 0), c_send.at[1, k])
        landed(at(0, 0), c_send.at[2, k])
    for r in range(2):
        landed(kv_at(0, r), e_send.at[r])
        for k in range(6):
            landed(far_b.at[0, lo], p_send.at[r, k])
    main.drain()
    outw.drain()
    keys.drain()


def per_device(residual_in, norm_gain, w_query, w_key_value, query_bias, key_value_bias, w_output, device_map, positions, segments):
    vec = jnp.concatenate([norm_gain, query_bias, key_value_bias]).astype(F32)[None, :]
    freq = (np.float64(ROPE_BASE) ** (-np.arange(HD // 2) * 2.0 / HD)).astype(np.float32)[:, None]
    freq = jnp.asarray(np.repeat(freq, TOK, axis=1))
    hbm = pl.BlockSpec(memory_space=pl.ANY)
    vm = pl.BlockSpec(memory_space=VM)
    turned = pl.pallas_call(
        layer,
        out_shape=jax.ShapeDtypeStruct((320, TOK), BF),
        in_specs=[pl.BlockSpec(memory_space=pltpu.SMEM), hbm, hbm, hbm, hbm, vm, vm, vm, vm],
        out_specs=vm,
        scratch_shapes=[
            VM((TOK, D), BF),
            VM((256, ROWS, TOK), F32),
            VM((640, TOK), F32),
            VM((TOK, D), BF),
            VM((16, ROWS, WC), BF),
            VM((80, WC), F32),
            VM((16, 320, WC), BF),
            VM((4, ROWS, 1024), BF),
            VM((80, 1024), F32),
            VM((16, 80, 1024), BF),
            VM((16, 1, TOK), jnp.int32),
            VM((16, TOK, HD), BF),
            VM((TOK, WC), F32),
            VM((2, TOK, HD), F32),
            VM((384, TOK), F32),
            VM((2, TOK, 256), BF),
            VM((16, TOK, 256), BF),
            VM((2, TOK, HD), F32),
            VM((2, TOK, 256), F32),
            VM((4, TOK, 256), BF),
        ]
        + [VM((2, 320, 256), BF)] * 6
        + [
            DMA((2, 16)), DMA((2, 16)), DMA((4,)), DMA((4,)), DMA((16,)), DMA((16,)),
            DMA((sends_of(4),)), DMA((16, 4)), DMA((sends_of(2),)), DMA((16, 2)), DMA((sends_of(4),)), DMA((16, 4)), DMA((2,)),
            DMA((3, 4)), DMA((4, 4)), DMA((2, 6)), DMA((2, 6)), DMA,
        ],
        compiler_params=pltpu.CompilerParams(collective_id=0, has_side_effects=True, vmem_limit_bytes=VLIM),
        name="layer",
    )(
        device_map, residual_in, w_query, w_key_value, w_output.T, vec,
        positions[None, :], segments[None, :], freq,
    )
    return turned.T


def solution(mesh):
    both = ("blk", "tp")
    placed = (P("blk", None), P(), P(both, None), P(both, None), P(), P(), P(None, both), P(), P("blk"), P("blk"))
    return jax.shard_map(per_device, mesh=mesh, in_specs=placed, out_specs=P("blk", "tp"), check_vma=False)
```

time: 326 us -> 129 us (0.40)
  Pallas kernels: 0 us -> 124 us
  waiting for transfers between devices: 119 us -> 0 us
  matrix products: 72.4 us -> 0 us
  local copies, waits for them, and re-layouts: 48.9 us -> 3.84 us
  other arithmetic: 28 us -> 0.67 us
  starting transfers between devices: 23.2 us -> 0 us
  blocking collectives: 17.7 us -> 0 us
  between operations: 13.5 us -> 0.02 us
    pallas_call x0 -> x1, Pallas kernels: none -> 124 us  [per_device(): pl.pallas_call(layer, out_shape=jax.ShapeDtypeStruct((320, TOK), BF), in_...]
    dot_general x35 -> x0, matrix products: 72.4 us -> none  [the longest x16 31.5 us: one_block(): jnp.einsum('hqk,kd->hqd', raw_weights.astype(jnp.bfloat16), value_block,...]
    reduce_scatter x1 -> x0, waiting for transfers between devices: 59.1 us -> none  [sum_by_axis(): nearer = lax.psum_scatter(x, axes[0], scatter_dimension=dim, tiled=True)]
    unnamed x6 -> x0, waiting for transfers between devices: 37.4 us -> none
    all_to_all x3 -> x0, starting transfers between devices: 20 us -> none  [the longest x1 11.2 us: per_device(): lax.all_to_all(w_key_value, TP, split_axis=1, concat_axis=0, tiled=True)]
    all_gather x1 -> x0, blocking collectives: 17.7 us -> none  [per_device(): lax.all_gather(segments, 'blk', axis=0, tiled=True)]
    gather x2 -> x0, local copies, waits for them, and re-layouts: 15.4 us -> none  [per_device(): jnp.take(normed.reshape(local_tokens, device_map.shape[0], shard_rows), d...]
    reduce_sum x17 -> x0, other arithmetic: 12.8 us -> none  [the longest x16 9.08 us: one_block(): run_mass = run_mass * factor + jnp.sum(raw_weights, axis=2)]
  transfers between devices with their start and end apart: 9 -> 0, of which waited for: 6 -> 0; matrix products, arithmetic and copies ran while one was open for 39% -> 0% of each run, Pallas kernels for 0% -> 0%
where the time goes in v2:
time: 129 us; the launch traced here: 128 us
  Pallas kernels  124 us (96%)
  local copies, waits for them, and re-layouts  3.84 us (3%)
    pallas_call x1, Pallas kernels, per_device(): pl.pallas_call(layer, out_shape=jax.ShapeDtypeStruct((320, TOK), BF), in_...  124 us

profile of v2, /device:TPU:6, one launch (start us, length us, event | category | flops | bytes accessed | tf_op | source)
XLA Modules:
  0.0 128.1 jit_solution(8219112518059845569)
XLA Ops:
  0.0 0.7 concatenate.18
  0.7 0.7 concatenate.17
  1.4 0.7 concatenate.16
  2.1 0.7 maximum_convert_fusion.vec
  2.8 123.6 %layer.1 = bf16[320,512]{1,0:T(8,128)(2,1)} custom-call(s32[256]{0:T(256)} %dm.1, bf16[512,5120]{1,0:T(8,128)(2,1)} %x_hbm.1, bf16[20,4096]{1,0:T(8,128)(2,1)} %wq.1, bf16[20,2048]{1,0:T(8,128)(2,1)} %wkv.1, bf16[20,4096]{1,0:T(8,128)(2,1)} %bitcast.5, f32[1,11264]{1,0:T(1,128)} %maximum_convert_fusion.vec, s32[1,512]{1,0:T(1,128)} %bitcast.6, ...), custom_call_target="tpu_custom_call" | custom-call | tf_op jit(solution)/shard_map/layer/pallas_call | solution.py:505
  126.4 1.7 %copy.13 = bf16[512,320]{0,1:T(8,128)(2,1)} copy(bf16[512,320]{0,1:T(8,128)(2,1)} %bitcast.4) | data formatting | bytes 655360

commit v3 on v2

--- a/solution.py
+++ b/solution.py
@@ -160,16 +160,16 @@
 
 
 def layer(
-    dm, x_hbm, wq, wkv, wo, vec, pos, seg, freq,
+    dm, x_hbm, wq, wkv, wo, gain_h, qb_h, kb_h, pos_h, seg_h, freq_h,
     out,
     xv, slot, five, ordered, land, wide, w, land_o, wide_o, wog, segs, kaug, acc_w, trig, res, q, kvg, m_s, acc_s, cg, far_b, plus, minus,
     r_far, r_plus, r_minus,
     a_send, a_recv, o_send, o_recv, s_send, s_recv, g_send, g_recv, h_send, h_recv, k_send, k_recv, e_send, c_send, c_recv, p_send, p_recv,
-    x_sem,
+    x_sem, gain, qb, kb, pos, seg, freq, gain_row, i_sem,
 ):
     b, t, x, zl, c, y, zh = coords()
     hl = t % 2
-    main = Gather(lambda k, p: w.at[k, pl.ds(p * 80, 80)], 4, g_send, g_recv)
+    main = Gather(lambda k, p: w.at[k, pl.ds(pl.multiple_of((zh + p) % 4 * 80, 80), 80)], 4, g_send, g_recv)
     outw = Gather(lambda k, p: wog.at[k, :, pl.ds(p * 512, 512)], 2, h_send, h_recv)
 
     def kv_at(k, p):
@@ -187,6 +187,12 @@
 
     x_copy = pltpu.make_async_copy(x_hbm, xv, x_sem)
     x_copy.start()
+    in_copy = [
+        pltpu.make_async_copy(src, dst, i_sem.at[k])
+        for k, (src, dst) in enumerate(((gain_h, gain), (qb_h, qb), (kb_h, kb), (pos_h, pos), (seg_h, seg), (freq_h, freq)))
+    ]
+    for copy in in_copy:
+        copy.start()
     for k in range(1, 16):
         signal({"blk": b, "tp": (t + k) % 16})
         signal({"blk": (b + k) % 16, "tp": t})
@@ -213,16 +219,23 @@
     def kv_land(k):
         return land.at[k, :, pl.ds(256, 128)]
 
-    for k in (4, 12, 1, 3, 5, 7, 13, 15, 8, 2, 9, 6, 14, 10, 11):
-        to = (t + k) % 16
+    for k in range(1, 16):
+        to = (y + k) % 4 * 4 + (zh + (0, 3, 1, 2)[k // 4]) % 4
         push(q_src(to), q_land(t), a_send.at[0, k], a_recv.at[0, t], {"blk": b, "tp": to})
         push(kv_src(to), kv_land(t), a_send.at[1, k], a_recv.at[1, t], {"blk": b, "tp": to})
     pltpu.make_async_copy(q_src(t), q_land(t), a_recv.at[0, t]).start()
     pltpu.make_async_copy(kv_src(t), kv_land(t), a_recv.at[1, t]).start()
-    for k in range(1, 16):
-        push(seg, segs.at[b], s_send.at[k], s_recv.at[b], {"blk": (b + k) % 16, "tp": t})
-    segs[b] = seg[...]
-
+
+    def send_segs():
+        in_copy[4].wait()
+        for k in range(1, 16):
+            push(seg, segs.at[b], s_send.at[k], s_recv.at[b], {"blk": (b + k) % 16, "tp": t})
+        segs[b] = seg[...]
+
+
+    in_copy[0].wait()
+    for k in range(D // 256):
+        gain_row[:, k * 256 : (k + 1) * 256] = gain[k * 256 : (k + 1) * 256].astype(F32)[None, :]
     x_copy.wait()
 
     def squares(j, acc):
@@ -236,7 +249,7 @@
     def turn(i, carry):
         for k in range(5):
             at = pl.ds(pl.multiple_of(i * 640 + k * 128, 128), 128)
-            v = xv[:, at].astype(F32) * trig[0] * vec[:, at]
+            v = xv[:, at].astype(F32) * trig[0] * gain_row[:, at]
             five[k * 128 : (k + 1) * 128, :] = v.astype(BF).astype(F32).T
         for k in range(32):
             slot[i * 32 + k] = five[k * ROWS : (k + 1) * ROWS, :]
@@ -246,17 +259,20 @@
 
     def back(i):
         for k in range(32):
-            five[k * ROWS : (k + 1) * ROWS, :] = slot[dm[i * 32 + k]]
+            f = k // 16 * 16 + k % 4 * 4 + k // 4 % 4
+            five[k * ROWS : (k + 1) * ROWS, :] = slot[dm[i * 32 + f]]
         for k in range(5):
             at = pl.ds(pl.multiple_of(i * 640 + k * 128, 128), 128)
             ordered[:, at] = five[k * 128 : (k + 1) * 128, :].T.astype(BF)
 
     def group(g):
+        zs = (zh + g) % 4
         for k in range(4):
-            landed(q_land(4 * g + k), a_recv.at[0, 4 * g + k])
-            landed(kv_land(4 * g + k), a_recv.at[1, 4 * g + k])
-            wide[k * ROWS : (k + 1) * ROWS, :] = land[4 * g + k].astype(F32)
-        w[b, pl.ds(g * 80, 80), :] = wide[...].astype(BF)
+            frm = 4 * k + zs
+            landed(q_land(frm), a_recv.at[0, frm])
+            landed(kv_land(frm), a_recv.at[1, frm])
+            wide[k * ROWS : (k + 1) * ROWS, :] = land[frm].astype(F32)
+        w[b, pl.ds(pl.multiple_of(zs * 80, 80), 80), :] = wide[...].astype(BF)
         main.mine(g)
 
     def send_out():
@@ -271,17 +287,20 @@
             def _():
                 pltpu.make_async_copy(src, land_o.at[zh], o_recv.at[zh]).start()
 
+    group(0)
     run(8, back, {
-        0: seq((group, 0)),
-        1: seq((group, 1)),
-        2: seq((group, 2), (main.zfwd, 0)),
-        3: seq((group, 3), (main.zfwd, 1)),
-        4: seq((send_out,), (main.zfwd, 2), (main.side, False, 0)),
-        5: seq((main.zfwd, 3), (main.side, False, 1)),
-        6: seq((main.side, False, 2)),
-        7: seq((main.side, False, 3)),
+        0: seq((group, 1)),
+        1: seq((group, 3), (main.zfwd, 0)),
+        2: seq((group, 2), (main.side, False, 0)),
+        3: seq((send_segs,), (send_out,), (main.zfwd, 1)),
+        4: seq((main.zfwd, 3), (main.side, False, 1)),
+        5: seq((main.zfwd, 2), (main.side, True, 0)),
+        6: seq((main.side, False, 3)),
+        7: seq((main.side, False, 2)),
     })
 
+    for k in (1, 2, 3, 5):
+        in_copy[k].wait()
     angle = freq[...] * pos[...].astype(F32)
     cos_t, sin_t = cos_sin(angle)
     trig[0] = jnp.concatenate([cos_t, cos_t], axis=0).T
@@ -309,18 +328,20 @@
             kaug[j] = jnp.where(row0, jnp.broadcast_to(row, (HD, TOK)), 0.0).T.astype(BF)
 
     run(8, mul, {
-        0: seq((main.side, True, 0, 1), (main.sibs, 0)),
-        1: seq((main.side, True, 2, 3), (main.sibs, 1)),
-        2: seq((main.far, False, 0, 1), (main.sibs, 2)),
-        3: seq((main.far, False, 2, 3), (main.sibs, 3)),
-        4: seq((main.sibs, 4),),
-        5: seq((main.far, True, 0, 1), (main.sibs, 5)),
-        6: seq((main.far, True, 2, 3), (main.sibs, 6)),
+        0: seq((main.far, False, 0), (main.side, True, 1), (main.sibs, 0)),
+        1: seq((main.far, False, 1), (main.side, True, 3), (main.sibs, 1)),
+        2: seq((main.side, True, 2), (main.far, False, 3), (main.sibs, 2)),
+        3: seq((main.far, False, 2), (main.far, True, 0), (main.sibs, 3)),
+        4: seq((main.far, True, 1), (main.sibs, 4)),
+        5: seq((main.far, True, 3), (main.sibs, 5)),
+        6: seq((main.far, True, 2), (main.sibs, 6)),
         7: seq((main.sibs, 7),),
     })
 
     is_key = hl == 0
-    kv_bias = vec[:, pl.ds(pl.multiple_of(D + 4096 + t * 128, 128), 128)]
+    kv_pair = kb[pl.ds(pl.multiple_of(t // 2 * 256, 256), 256)].astype(F32)[None, :]
+    kv_bias = jnp.where(is_key, kv_pair[:, :HD], kv_pair[:, HD:])
+    q_bias = qb[pl.ds(pl.multiple_of(t * 256, 256), 256)].astype(F32)[None, :]
     u = acc_w[:, 256:384] + kv_bias
     turned = u * trig[0] + pltpu.roll(u, HD // 2, 1) * trig[1]
     mine = pl.ds(pl.multiple_of(hl * 128, 128), 128)
@@ -331,41 +352,45 @@
         keys.mine(r)
     own_seg = jnp.where(row0, jnp.broadcast_to(seg[...].astype(F32), (HD, TOK)), 0.0).T.astype(BF)
     for h in range(2):
-        q_bias = vec[:, pl.ds(pl.multiple_of(D + t * 256 + h * 128, 128), 128)]
-        u = acc_w[:, h * HD : (h + 1) * HD] + q_bias
-        q[h, :, 0:HD] = (u * trig[0] + pltpu.roll(u, HD // 2, 1) * trig[1]).astype(BF)
-        q[h, :, HD:] = own_seg
+        u = acc_w[:, h * HD : (h + 1) * HD] + q_bias[:, h * HD : (h + 1) * HD]
+        u = (u * trig[0] + pltpu.roll(u, HD // 2, 1) * trig[1]).astype(BF)
+        for r in range(2):
+            q[r, h * 256 : (h + 1) * 256, 0:HD] = u[r * 256 : (r + 1) * 256]
+            q[r, h * 256 : (h + 1) * 256, HD:] = own_seg[r * 256 : (r + 1) * 256]
 
     coef = HD ** -0.5 * LOG2E
     half = TOK // 2
 
-    def block(j, diagonal):
-        kop = jnp.concatenate([kvg[j, :, 0:HD], kaug[j]], axis=1)
-        vop = jnp.concatenate([kvg[j, :, HD:], jnp.ones((TOK, HD), BF)], axis=1)
-        for h in range(2):
-            for r in range(2):
-                rows = pl.ds(r * half, half)
-                s = lax.dot_general(q[h, rows, :], kop, (((1,), (1,)), ((), ())), preferred_element_type=F32)
-                if diagonal:
-                    qi = lax.broadcasted_iota(jnp.int32, s.shape, 0) + r * half
-                    ki = lax.broadcasted_iota(jnp.int32, s.shape, 1)
-                    s = jnp.where(ki <= qi, s, NEGATIVE_FILL)
-                peak = jnp.max(s, axis=1, keepdims=True)
-                if diagonal:
-                    new = peak
-                else:
-                    old = m_s[h, rows, :]
-                    new = jnp.maximum(old, peak)
-                    factor = jnp.exp2((old - new) * coef)
-                e = jnp.exp2(s * coef - (new * coef)[:, 0:1]).astype(BF)
-                o = jnp.dot(e, vop, preferred_element_type=F32)
-                if diagonal:
-                    m_s[h, rows, :] = jnp.broadcast_to(new, (half, HD))
-                    acc_s[h, rows, :] = o
-                else:
-                    m_s[h, rows, :] = new
-                    acc_s[h, rows, 0:HD] = acc_s[h, rows, 0:HD] * factor + o[:, 0:HD]
-                    acc_s[h, rows, HD:] = acc_s[h, rows, HD:] * factor + o[:, HD:]
+    def block(pair, r, first):
+        ss = []
+        for k in range(2):
+            j = 2 * pair + k
+            kop = jnp.concatenate([kvg[j, :, 0:HD], kaug[j]], axis=1)
+            v = lax.dot_general(q[r], kop, (((1,), (1,)), ((), ())), preferred_element_type=F32)
+            if first:
+                qi = lax.broadcasted_iota(jnp.int32, (TOK, TOK), 0) % half + r * half + c * TOK
+                ki = lax.broadcasted_iota(jnp.int32, (TOK, TOK), 1) + k * TOK
+                v = jnp.where(ki <= qi, v, NEGATIVE_FILL)
+            ss += [v[:, i * HD : (i + 1) * HD] for i in range(4)]
+        top = ss
+        while len(top) > 1:
+            top = [jnp.maximum(top[i], top[i + 1]) for i in range(0, len(top), 2)]
+        new = jnp.broadcast_to(jnp.max(top[0], axis=1, keepdims=True), (TOK, HD))
+        if not first:
+            old = m_s[r]
+            new = jnp.maximum(old, new)
+            factor = jnp.exp2((old - new) * coef)
+        o = jnp.zeros((TOK, 2 * HD), F32)
+        for k in range(2):
+            e = jnp.concatenate([jnp.exp2((ss[4 * k + i] - new) * coef).astype(BF) for i in range(4)], axis=1)
+            vop = jnp.concatenate([kvg[2 * pair + k, :, HD:], jnp.ones((TOK, HD), BF)], axis=1)
+            o = o + jnp.dot(e, vop, preferred_element_type=F32)
+        m_s[r] = new
+        if first:
+            acc_s[r] = o
+        else:
+            acc_s[r, :, 0:HD] = acc_s[r, :, 0:HD] * factor + o[:, 0:HD]
+            acc_s[r, :, HD:] = acc_s[r, :, HD:] * factor + o[:, HD:]
 
     def squeeze_out():
         for k in range(4):
@@ -379,33 +404,28 @@
         keys.wait(b, 2 + r)
         keys.mine(2 + r)
     squeeze_out()
-    block(b, True)
+    keys.sibs(0)
+    block(b // 2, 0, True)
     keys.zfwd(2, 3)
 
-    def visit(i):
-        chunk = pick(keys.order, i // 2)
-        chunk = jnp.where(i % 2 == 1, flip(chunk), chunk)
-
-        @pl.when(chunk < b)
-        def _():
-            block(chunk, False)
-
-    run(16, visit, {
-        0: seq((keys.side, False, 2, 3)),
-        1: seq((keys.side, True, 0, 1), (keys.sibs, 0)),
-        3: seq((keys.sibs, 1),),
-        4: seq((keys.side, True, 2, 3)),
-        5: seq((keys.sibs, 2),),
-        6: seq((keys.far, False, 0, 1)),
-        7: seq((keys.sibs, 3),),
-        8: seq((outw.mine, 0, 1)),
-        9: seq((keys.far, False, 2, 3), (keys.sibs, 4)),
-        10: seq((keys.far, True, 0, 1)),
-        11: seq((keys.sibs, 5), (outw.zfwd, 0, 1)),
-        12: seq((keys.far, True, 2, 3)),
-        13: seq((keys.sibs, 6), (outw.side, False, 0, 1)),
-        14: seq((outw.side, True, 0, 1)),
-        15: seq((keys.sibs, 7),),
+    def visit(r):
+        def go(i):
+            pair = pick(keys.order[1:], i) // 2
+
+            @pl.when(pair < b // 2)
+            def _():
+                block(pair, r, False)
+
+        return go
+
+    run(7, visit(0), {
+        0: seq((keys.side, False, 2, 3), (keys.side, True, 0, 1), (keys.sibs, 1)),
+        1: seq((keys.far, False, 0, 1), (keys.sibs, 2)),
+        2: seq((keys.side, True, 2, 3), (keys.sibs, 3)),
+        3: seq((keys.far, True, 0, 1), (keys.far, False, 2, 3), (keys.sibs, 4)),
+        4: seq((keys.sibs, 5),),
+        5: seq((keys.far, True, 2, 3), (outw.mine, 0, 1), (keys.sibs, 6)),
+        6: seq((keys.sibs, 7),),
     })
 
     up, down, opp = (zh + 1) % 4, (zh + 3) % 4, (zh + 2) % 4
@@ -417,20 +437,31 @@
     def waitc(k, p):
         landed(at(k, p), c_recv.at[k, p])
 
-    for r in range(2):
+    def mine_c(r):
         rows = pl.ds(r * half, half)
         for h in range(2):
-            cg[zh, rows, h * HD : (h + 1) * HD] = (acc_s[h, rows, 0:HD] / acc_s[h, rows, HD:]).astype(BF)
+            hr = pl.ds(h * half, half)
+            cg[zh, rows, h * HD : (h + 1) * HD] = (acc_s[r, hr, 0:HD] / acc_s[r, hr, HD:]).astype(BF)
         for p in (2 * r, 2 * r + 1):
             push(at(zh, p), at(zh, p), c_send.at[0, p], c_recv.at[zh, p], zdev(up))
             push(at(zh, p), at(zh, p), c_send.at[1, p], c_recv.at[zh, p], zdev(down))
-        if r == 0:
-            outw.far(False, 0, 1)
+
+    def fwd_c(r):
         waitc(down, 2 * r)
         push(at(down, 2 * r), at(down, 2 * r), c_send.at[2, 2 * r], c_recv.at[down, 2 * r], zdev(up))
         waitc(up, 2 * r + 1)
         push(at(up, 2 * r + 1), at(up, 2 * r + 1), c_send.at[2, 2 * r + 1], c_recv.at[up, 2 * r + 1], zdev(down))
-    outw.far(True, 0, 1)
+
+    mine_c(0)
+    outw.zfwd(0, 1)
+    block(b // 2, 1, True)
+    run(7, visit(1), {
+        1: seq((outw.side, False, 0, 1)),
+        3: seq((fwd_c, 0), (outw.side, True, 0, 1)),
+        5: seq((outw.far, False, 0, 1)),
+        6: seq((outw.far, True, 0, 1)),
+    })
+    mine_c(1)
     for k in range(8):
         outw.sibs(k)
 
@@ -446,7 +477,9 @@
         return v
 
     lo, hi = pl.ds(0, 160), pl.ds(160, 160)
-    for r in range(2):
+    kept = {}
+
+    def scatter_far(r):
         waitc(down, 2 * r + 1)
         waitc(up, 2 * r)
         waitc(opp, 2 * r)
@@ -460,20 +493,37 @@
         u = partial(ym, r)
         minus[r, lo, :] = u[:160].astype(BF)
         push(minus.at[r, lo], r_minus.at[r, lo], p_send.at[r, 3], p_recv.at[r, 3], ydev(ym))
+        kept[r] = v[:160], u[160:]
+
+    def scatter_near(r):
+        v, u = kept[r]
         landed(r_far.at[r, lo], p_recv.at[r, 0])
-        plus[r, lo, :] = (v[:160] + r_far[r, lo, :].astype(F32)).astype(BF)
+        plus[r, lo, :] = (v + r_far[r, lo, :].astype(F32)).astype(BF)
         push(plus.at[r, lo], r_plus.at[r, lo], p_send.at[r, 4], p_recv.at[r, 4], ydev(yp))
         landed(r_far.at[r, hi], p_recv.at[r, 1])
-        minus[r, hi, :] = (u[160:] + r_far[r, hi, :].astype(F32)).astype(BF)
+        minus[r, hi, :] = (u + r_far[r, hi, :].astype(F32)).astype(BF)
         push(minus.at[r, hi], r_minus.at[r, hi], p_send.at[r, 5], p_recv.at[r, 5], ydev(ym))
+
+    def keep(r):
         cols = pl.ds(r * half, half)
         res[pl.ds(0, 320), cols] = partial(y, r) + res[pl.ds(pl.multiple_of(64 * hl, 64), 320), cols]
-    for r in range(2):
+
+    def finish(r):
         for sl, k1, k2 in ((hi, 2, 5), (lo, 4, 3)):
             landed(r_plus.at[r, sl], p_recv.at[r, k1])
             landed(r_minus.at[r, sl], p_recv.at[r, k2])
         cols = pl.ds(r * half, half)
         out[:, cols] = (res[pl.ds(0, 320), cols] + r_plus[r].astype(F32) + r_minus[r].astype(F32)).astype(BF)
+
+    scatter_far(0)
+    keep(0)
+    scatter_near(0)
+    fwd_c(1)
+    scatter_far(1)
+    keep(1)
+    scatter_near(1)
+    finish(0)
+    finish(1)
 
     for k in range(1, 16):
         landed(q_land(0), a_send.at[0, k])
@@ -497,7 +547,6 @@
 
 
 def per_device(residual_in, norm_gain, w_query, w_key_value, query_bias, key_value_bias, w_output, device_map, positions, segments):
-    vec = jnp.concatenate([norm_gain, query_bias, key_value_bias]).astype(F32)[None, :]
     freq = (np.float64(ROPE_BASE) ** (-np.arange(HD // 2) * 2.0 / HD)).astype(np.float32)[:, None]
     freq = jnp.asarray(np.repeat(freq, TOK, axis=1))
     hbm = pl.BlockSpec(memory_space=pl.ANY)
@@ -505,7 +554,7 @@
     turned = pl.pallas_call(
         layer,
         out_shape=jax.ShapeDtypeStruct((320, TOK), BF),
-        in_specs=[pl.BlockSpec(memory_space=pltpu.SMEM), hbm, hbm, hbm, hbm, vm, vm, vm, vm],
+        in_specs=[pl.BlockSpec(memory_space=pltpu.SMEM), hbm, hbm, hbm, hbm, hbm, hbm, hbm, hbm, hbm, hbm],
         out_specs=vm,
         scratch_shapes=[
             VM((TOK, D), BF),
@@ -534,11 +583,13 @@
             DMA((2, 16)), DMA((2, 16)), DMA((4,)), DMA((4,)), DMA((16,)), DMA((16,)),
             DMA((sends_of(4),)), DMA((16, 4)), DMA((sends_of(2),)), DMA((16, 2)), DMA((sends_of(4),)), DMA((16, 4)), DMA((2,)),
             DMA((3, 4)), DMA((4, 4)), DMA((2, 6)), DMA((2, 6)), DMA,
+            VM((D,), BF), VM((4096,), BF), VM((2048,), BF), VM((1, TOK), jnp.int32), VM((1, TOK), jnp.int32), VM((HD // 2, TOK), F32), VM((1, D), F32),
+            DMA((6,)),
         ],
         compiler_params=pltpu.CompilerParams(collective_id=0, has_side_effects=True, vmem_limit_bytes=VLIM),
         name="layer",
     )(
-        device_map, residual_in, w_query, w_key_value, w_output.T, vec,
+        device_map, residual_in, w_query, w_key_value, w_output.T, norm_gain, query_bias, key_value_bias,
         positions[None, :], segments[None, :], freq,
     )
     return turned.T

time: 129 us -> 111 us (0.86)
  Pallas kernels: 124 us -> 109 us
  local copies, waits for them, and re-layouts: 3.84 us -> 1.72 us
    pallas_call x1, Pallas kernels: 124 us -> 109 us  [per_device(): pl.pallas_call(layer, out_shape=jax.ShapeDtypeStruct((320, TOK), BF), in_...]
    concatenate x3 -> x0, local copies, waits for them, and re-layouts: 2.12 us -> none  [per_device(): jnp.concatenate([norm_gain, query_bias, key_value_bias]).astype(F32)]
where the time goes in v3:
time: 111 us; the launch traced here: 110 us
  Pallas kernels  109 us (98%)
  local copies, waits for them, and re-layouts  1.72 us (2%)
    pallas_call x1, Pallas kernels, per_device(): pl.pallas_call(layer, out_shape=jax.ShapeDtypeStruct((320, TOK), BF), in_...  109 us

profile of v3, /device:TPU:6, one launch (start us, length us, event | category | flops | bytes accessed | tf_op | source)
XLA Modules:
  0.0 110.4 jit_solution(8883301865063223929)
XLA Ops:
  0.0 108.7 %layer.1 = bf16[320,512]{1,0:T(8,128)(2,1)} custom-call(s32[256]{0:T(256)} %dm.1, bf16[512,5120]{1,0:T(8,128)(2,1)} %x_hbm.1, bf16[20,4096]{1,0:T(8,128)(2,1)} %wq.1, bf16[20,2048]{1,0:T(8,128)(2,1)} %wkv.1, bf16[20,4096]{1,0:T(8,128)(2,1)} %bitcast.5, bf16[5120]{0:T(1024)(128)(2,1)} %gain_h.1, bf16[4096]{0:T(1024)(128)(2,1)} %qb_h.1, bf16[2048]{0:T(1024)(128)(2,1)} %kb_h.1, ...), custom_call_target="tpu_custom_call" | custom-call | tf_op jit(solution)/shard_map/layer/pallas_call | solution.py:554
  108.7 1.7 %copy.13 = bf16[512,320]{0,1:T(8,128)(2,1)} copy(bf16[512,320]{0,1:T(8,128)(2,1)} %bitcast.4) | data formatting | bytes 655360

commit v4 on v3

--- a/solution.py
+++ b/solution.py
@@ -51,8 +51,8 @@
 
 
 class Gather:
-    def __init__(self, at, pieces, send, recv):
-        self.at, self.n, self.send, self.recv = at, pieces, send, recv
+    def __init__(self, at, pieces, send, recv, xfirst=()):
+        self.at, self.n, self.send, self.recv, self.xfirst = at, pieces, send, recv, xfirst
         b, t, x, zl, c, y, zh = coords()
         self.t = t
         self.own = b
@@ -76,33 +76,55 @@
     def wait(self, chunk, p):
         landed(self.at(chunk, p), self.recv.at[chunk, p])
 
+    def own_z(self, *pieces):
+        for p in pieces:
+            for to in (self.z, self.sib):
+                self._send(self.own, p, to)
+
+    def own_x(self, *pieces):
+        for p in pieces:
+            for to in (self.xp, self.xm):
+                self._send(self.own, p, to)
+
     def mine(self, *pieces):
         for p in pieces:
-            for to in (self.xp, self.xm, self.z, self.sib):
-                self._send(self.own, p, to)
+            self.own_x(p)
+            self.own_z(p)
+
+    def z_in(self, *pieces):
+        for p in pieces:
+            self.wait(self.z, p)
+            self._send(self.z, p, self.sib)
+
+    def z_out(self, *pieces):
+        for p in pieces:
+            for to in (self.xp, self.xm):
+                self._send(self.z, p, to)
 
     def zfwd(self, *pieces):
         for p in pieces:
             self.wait(self.z, p)
-            for to in (self.xp, self.xm, self.sib):
-                self._send(self.z, p, to)
+            if p not in self.xfirst:
+                self.z_out(p)
+            self._send(self.z, p, self.sib)
 
     def side(self, zside, *pieces):
         minus, plus = (self.xmz, self.xpz) if zside else (self.xm, self.xp)
         for p in pieces:
-            self.wait(minus, p)
-            if p % 2 == 0:
-                self._send(minus, p, self.xp)
-            self._send(minus, p, self.sib)
-            self.wait(plus, p)
-            if p % 2 == 1:
-                self._send(plus, p, self.xm)
-            self._send(plus, p, self.sib)
+            for chunk, on, even in ((minus, self.xp, 0), (plus, self.xm, 1)):
+                self.wait(chunk, p)
+                if p % 2 == even and not (zside and p in self.xfirst):
+                    self._send(chunk, p, on)
+                if p in self.xfirst and not zside:
+                    self._send(chunk, p, self.z)
+                self._send(chunk, p, self.sib)
 
     def far(self, zside, *pieces):
         chunk = self.x2z if zside else self.x2
         for p in pieces:
             self.wait(chunk, p)
+            if p in self.xfirst and not zside:
+                self._send(chunk, p, self.z)
             self._send(chunk, p, self.sib)
 
     def sibs(self, k):
@@ -162,12 +184,13 @@
 def layer(
     dm, x_hbm, wq, wkv, wo, gain_h, qb_h, kb_h, pos_h, seg_h, freq_h,
     out,
-    xv, slot, five, ordered, land, wide, w, land_o, wide_o, wog, segs, kaug, acc_w, trig, res, q, kvg, m_s, acc_s, cg, far_b, plus, minus,
-    r_far, r_plus, r_minus,
+    xv, slot, five, ordered, land, wide, w, land_o, wide_o, wog, segs, kaug, acc_w, trig, res, q, kvg, m_s, acc_s, cg,
+    fb0, pb0, mb0, rf0, rp0, rm0, fb1, pb1, mb1, rf1, rp1, rm1,
     a_send, a_recv, o_send, o_recv, s_send, s_recv, g_send, g_recv, h_send, h_recv, k_send, k_recv, e_send, c_send, c_recv, p_send, p_recv,
     x_sem, gain, qb, kb, pos, seg, freq, gain_row, i_sem,
 ):
     b, t, x, zl, c, y, zh = coords()
+    wide_bufs, narrow_bufs = (fb0, pb0, mb0, rf0, rp0, rm0), (fb1, pb1, mb1, rf1, rp1, rm1)
     hl = t % 2
     main = Gather(lambda k, p: w.at[k, pl.ds(pl.multiple_of((zh + p) % 4 * 80, 80), 80)], 4, g_send, g_recv)
     outw = Gather(lambda k, p: wog.at[k, :, pl.ds(p * 512, 512)], 2, h_send, h_recv)
@@ -238,13 +261,17 @@
         gain_row[:, k * 256 : (k + 1) * 256] = gain[k * 256 : (k + 1) * 256].astype(F32)[None, :]
     x_copy.wait()
 
-    def squares(j, acc):
-        v = xv[:, pl.ds(pl.multiple_of(j * 128, 128), 128)].astype(F32)
-        return acc + v * v
-
-    total = lax.fori_loop(0, D // 128, squares, jnp.zeros((TOK, 128), F32))
-    square = jnp.maximum(jnp.sum(total, axis=1, keepdims=True) * (1.0 / D), NORM_FLOOR)
-    trig[0] = jnp.broadcast_to(lax.rsqrt(square), (TOK, 128))
+    def squares(i, carry):
+        rows = pl.ds(pl.multiple_of(i * 64, 64), 64)
+        total = jnp.zeros((64, 128), F32)
+        for j in range(D // 128):
+            v = xv[rows, j * 128 : (j + 1) * 128].astype(F32)
+            total = total + v * v
+        square = jnp.maximum(jnp.sum(total, axis=1, keepdims=True) * (1.0 / D), NORM_FLOOR)
+        trig[0, rows, :] = jnp.broadcast_to(lax.rsqrt(square), (64, 128))
+        return carry
+
+    lax.fori_loop(0, TOK // 64, squares, 0)
 
     def turn(i, carry):
         for k in range(5):
@@ -262,8 +289,7 @@
             f = k // 16 * 16 + k % 4 * 4 + k // 4 % 4
             five[k * ROWS : (k + 1) * ROWS, :] = slot[dm[i * 32 + f]]
         for k in range(5):
-            at = pl.ds(pl.multiple_of(i * 640 + k * 128, 128), 128)
-            ordered[:, at] = five[k * 128 : (k + 1) * 128, :].T.astype(BF)
+            ordered[:, k * 128 : (k + 1) * 128] = five[k * 128 : (k + 1) * 128, :].T.astype(BF)
 
     def group(g):
         zs = (zh + g) % 4
@@ -287,17 +313,21 @@
             def _():
                 pltpu.make_async_copy(src, land_o.at[zh], o_recv.at[zh]).start()
 
+    def squeeze_out():
+        for k in range(4):
+            landed(land_o.at[k], o_recv.at[k])
+            wide_o[k * ROWS : (k + 1) * ROWS, :] = land_o[k].astype(F32)
+        wog[b] = wide_o[...].astype(BF)
+        outw.own_z(0, 1)
+
     group(0)
-    run(8, back, {
-        0: seq((group, 1)),
-        1: seq((group, 3), (main.zfwd, 0)),
-        2: seq((group, 2), (main.side, False, 0)),
-        3: seq((send_segs,), (send_out,), (main.zfwd, 1)),
-        4: seq((main.zfwd, 3), (main.side, False, 1)),
-        5: seq((main.zfwd, 2), (main.side, True, 0)),
-        6: seq((main.side, False, 3)),
-        7: seq((main.side, False, 2)),
-    })
+    group(1)
+    main.zfwd(0)
+    group(3)
+    group(2)
+    send_segs()
+    send_out()
+    acc_w[...] = jnp.zeros((TOK, WC), F32)
 
     for k in (1, 2, 3, 5):
         in_copy[k].wait()
@@ -308,35 +338,24 @@
     window = pl.ds(pl.multiple_of(128 * ((5 * t) // 2), 128), 384)
     res[...] = xv[:, window].astype(F32).T
 
-    acc_w[...] = jnp.zeros((TOK, WC), F32)
-    row0 = lax.broadcasted_iota(jnp.int32, (HD, TOK), 0) == 0
 
     def mul(i):
         pair = pick(main.order, i) // 2
-        lanes = pl.ds(pl.multiple_of(pair * 640, 640), 640)
-        acc_w[...] += jnp.dot(
-            ordered[:, lanes], w[pl.ds(pair * 2, 2)].reshape(640, WC), preferred_element_type=F32
-        )
-        for k in range(2):
-            j = 2 * i + k
-
-            @pl.when(j != b)
-            def _():
-                landed(segs.at[j], s_recv.at[j])
-
-            row = jnp.where(segs[j] == 0, NEGATIVE_FILL, 0.0)
-            kaug[j] = jnp.where(row0, jnp.broadcast_to(row, (HD, TOK)), 0.0).T.astype(BF)
+        back(pair)
+        acc_w[...] += jnp.dot(ordered[...], w[pl.ds(pair * 2, 2)].reshape(640, WC), preferred_element_type=F32)
 
     run(8, mul, {
-        0: seq((main.far, False, 0), (main.side, True, 1), (main.sibs, 0)),
-        1: seq((main.far, False, 1), (main.side, True, 3), (main.sibs, 1)),
-        2: seq((main.side, True, 2), (main.far, False, 3), (main.sibs, 2)),
-        3: seq((main.far, False, 2), (main.far, True, 0), (main.sibs, 3)),
-        4: seq((main.far, True, 1), (main.sibs, 4)),
-        5: seq((main.far, True, 3), (main.sibs, 5)),
-        6: seq((main.far, True, 2), (main.sibs, 6)),
-        7: seq((main.sibs, 7),),
+        0: seq((main.side, False, 0), (main.zfwd, 1), (main.sibs, 0)),
+        1: seq((main.zfwd, 3), (main.zfwd, 2), (main.side, False, 1), (main.sibs, 1)),
+        2: seq((main.side, True, 0), (main.side, False, 3), (main.side, False, 2), (main.sibs, 2)),
+        3: seq((main.far, False, 0), (main.side, True, 1), (main.sibs, 3)),
+        4: seq((main.far, False, 1), (main.side, True, 3), (main.side, True, 2), (main.sibs, 4)),
+        5: seq((main.far, False, 3), (main.far, False, 2), (squeeze_out,), (main.sibs, 5)),
+        6: seq((main.far, True, 0), (main.far, True, 1), (main.sibs, 6)),
+        7: seq((main.far, True, 3), (main.far, True, 2), (main.sibs, 7)),
     })
+
+    line = lax.broadcasted_iota(jnp.int32, (HD, TOK), 0)
 
     is_key = hl == 0
     kv_pair = kb[pl.ds(pl.multiple_of(t // 2 * 256, 256), 256)].astype(F32)[None, :]
@@ -350,7 +369,8 @@
     for r in range(2):
         push(kv_at(b, r), kv_at(b, r), e_send.at[r], k_recv.at[b, 2 + r], partner)
         keys.mine(r)
-    own_seg = jnp.where(row0, jnp.broadcast_to(seg[...].astype(F32), (HD, TOK)), 0.0).T.astype(BF)
+    own_seg = jnp.broadcast_to(seg[...].astype(F32), (HD, TOK))
+    own_seg = jnp.where(line == 0, own_seg, jnp.where(line == 1, 1.0, 0.0)).T.astype(BF)
     for h in range(2):
         u = acc_w[:, h * HD : (h + 1) * HD] + q_bias[:, h * HD : (h + 1) * HD]
         u = (u * trig[0] + pltpu.roll(u, HD // 2, 1) * trig[1]).astype(BF)
@@ -360,6 +380,20 @@
 
     coef = HD ** -0.5 * LOG2E
     half = TOK // 2
+
+    def column(j, carry):
+        @pl.when(j != b)
+        def _():
+            landed(segs.at[j], s_recv.at[j])
+
+        row = jnp.where(segs[j] == 0, NEGATIVE_FILL, 0.0)
+        later = jnp.where(j // 2 > b // 2, NEGATIVE_FILL, 0.0)
+        kaug[j] = jnp.where(
+            line == 0, jnp.broadcast_to(row, (HD, TOK)), jnp.where(line == 1, later, 0.0)
+        ).T.astype(BF)
+        return carry
+
+    lax.fori_loop(0, 16, column, 0)
 
     def block(pair, r, first):
         ss = []
@@ -392,47 +426,39 @@
             acc_s[r, :, 0:HD] = acc_s[r, :, 0:HD] * factor + o[:, 0:HD]
             acc_s[r, :, HD:] = acc_s[r, :, HD:] * factor + o[:, HD:]
 
-    def squeeze_out():
-        for k in range(4):
-            landed(land_o.at[k], o_recv.at[k])
-            wide_o[k * ROWS : (k + 1) * ROWS, :] = land_o[k].astype(F32)
-        wog[b] = wide_o[...].astype(BF)
-
-    keys.zfwd(0, 1)
     keys.side(False, 0, 1)
     for r in range(2):
         keys.wait(b, 2 + r)
         keys.mine(2 + r)
-    squeeze_out()
+    keys.zfwd(0, 1)
     keys.sibs(0)
     block(b // 2, 0, True)
+    block(b // 2, 1, True)
     keys.zfwd(2, 3)
-
-    def visit(r):
-        def go(i):
-            pair = pick(keys.order[1:], i) // 2
-
-            @pl.when(pair < b // 2)
-            def _():
-                block(pair, r, False)
-
-        return go
-
-    run(7, visit(0), {
-        0: seq((keys.side, False, 2, 3), (keys.side, True, 0, 1), (keys.sibs, 1)),
-        1: seq((keys.far, False, 0, 1), (keys.sibs, 2)),
-        2: seq((keys.side, True, 2, 3), (keys.sibs, 3)),
-        3: seq((keys.far, True, 0, 1), (keys.far, False, 2, 3), (keys.sibs, 4)),
-        4: seq((keys.sibs, 5),),
-        5: seq((keys.far, True, 2, 3), (outw.mine, 0, 1), (keys.sibs, 6)),
-        6: seq((keys.sibs, 7),),
-    })
+    keys.side(False, 2, 3)
+    keys.side(True, 0, 1)
+    keys.sibs(1)
+
+    @pl.when(keys.z < b)
+    def _():
+        block(keys.z // 2, 0, False)
+        block(keys.z // 2, 1, False)
+
+    def double(i):
+        one = pick(keys.order[2::2], i % 3) // 2
+        two = pick(keys.order[3::2], i % 3) // 2
+
+        @pl.when(jnp.minimum(one, two) < b // 2)
+        def _():
+            block(one, i // 3, False)
+            block(two, i // 3, False)
 
     up, down, opp = (zh + 1) % 4, (zh + 3) % 4, (zh + 2) % 4
     yp, ym, y2 = (y + 1) % 4, (y + 3) % 4, (y + 2) % 4
     zdev = lambda k: {"blk": b, "tp": y * 4 + k}
     ydev = lambda k: {"blk": b, "tp": k * 4 + zh}
-    at = lambda k, p: cg.at[k, pl.ds(p * 128, 128)]
+    at = lambda k, p: cg.at[k, pl.ds(p * 64, 64)]
+    part = TOK // 4
 
     def waitc(k, p):
         landed(at(k, p), c_recv.at[k, p])
@@ -442,35 +468,45 @@
         for h in range(2):
             hr = pl.ds(h * half, half)
             cg[zh, rows, h * HD : (h + 1) * HD] = (acc_s[r, hr, 0:HD] / acc_s[r, hr, HD:]).astype(BF)
-        for p in (2 * r, 2 * r + 1):
+        for p in range(4 * r, 4 * r + 4):
             push(at(zh, p), at(zh, p), c_send.at[0, p], c_recv.at[zh, p], zdev(up))
             push(at(zh, p), at(zh, p), c_send.at[1, p], c_recv.at[zh, p], zdev(down))
 
-    def fwd_c(r):
-        waitc(down, 2 * r)
-        push(at(down, 2 * r), at(down, 2 * r), c_send.at[2, 2 * r], c_recv.at[down, 2 * r], zdev(up))
-        waitc(up, 2 * r + 1)
-        push(at(up, 2 * r + 1), at(up, 2 * r + 1), c_send.at[2, 2 * r + 1], c_recv.at[up, 2 * r + 1], zdev(down))
-
-    mine_c(0)
-    outw.zfwd(0, 1)
-    block(b // 2, 1, True)
-    run(7, visit(1), {
-        1: seq((outw.side, False, 0, 1)),
-        3: seq((fwd_c, 0), (outw.side, True, 0, 1)),
-        5: seq((outw.far, False, 0, 1)),
-        6: seq((outw.far, True, 0, 1)),
+    def fwd_c(*quarters):
+        for r in quarters:
+            waitc(down, 2 * r)
+            push(at(down, 2 * r), at(down, 2 * r), c_send.at[2, 2 * r], c_recv.at[down, 2 * r], zdev(up))
+            waitc(up, 2 * r + 1)
+            push(at(up, 2 * r + 1), at(up, 2 * r + 1), c_send.at[2, 2 * r + 1], c_recv.at[up, 2 * r + 1], zdev(down))
+
+    run(6, double, {
+        0: seq((keys.side, True, 2), (keys.far, False, 0, 1), (keys.sibs, 2), (keys.sibs, 3)),
+        1: seq((keys.side, True, 3), (keys.far, False, 2, 3), (keys.far, True, 0), (keys.sibs, 4), (keys.sibs, 5)),
+        2: seq((keys.far, True, 1, 2, 3), (outw.z_in, 0, 1), (outw.own_x, 0, 1), (outw.z_out, 0, 1), (keys.sibs, 6), (keys.sibs, 7)),
+        3: seq((mine_c, 0),),
+        4: seq((outw.side, False, 0, 1)),
+        5: seq((fwd_c, 0), (outw.side, True, 0, 1)),
     })
     mine_c(1)
+    fwd_c(1)
+    outw.far(False, 0, 1)
+    outw.far(True, 0, 1)
     for k in range(8):
         outw.sibs(k)
 
+    parts = ((0, 256), (256, 128), (384, 128))
+    far_b, plus, minus, r_far, r_plus, r_minus = [
+        [wide_buf] + [narrow_buf.at[k] for k in range(2)]
+        for wide_buf, narrow_buf in zip(wide_bufs, narrow_bufs)
+    ]
+
     def partial(k, r):
-        v = jnp.zeros((320, half), F32)
+        start, n = parts[r]
+        v = jnp.zeros((320, n), F32)
         for i in range(4):
             v = v + lax.dot_general(
                 wog[pl.ds(k * 4, 4), :, i * 256 : (i + 1) * 256].reshape(320, 256),
-                cg[i, pl.ds(r * half, half), :],
+                cg[i, pl.ds(start, n), :],
                 (((1,), (1,)), ((), ())),
                 preferred_element_type=F32,
             )
@@ -480,50 +516,61 @@
     kept = {}
 
     def scatter_far(r):
-        waitc(down, 2 * r + 1)
-        waitc(up, 2 * r)
-        waitc(opp, 2 * r)
-        waitc(opp, 2 * r + 1)
-        far_b[r] = partial(y2, r).astype(BF)
-        push(far_b.at[r, lo], r_far.at[r, lo], p_send.at[r, 0], p_recv.at[r, 0], ydev(yp))
-        push(far_b.at[r, hi], r_far.at[r, hi], p_send.at[r, 1], p_recv.at[r, 1], ydev(ym))
+        for k in ((0, 1), (2,), (3,))[r]:
+            waitc(down, 2 * k + 1)
+            waitc(up, 2 * k)
+            waitc(opp, 2 * k)
+            waitc(opp, 2 * k + 1)
+        far_b[r][...] = partial(y2, r).astype(BF)
+        push(far_b[r].at[lo], r_far[r].at[lo], p_send.at[r, 0], p_recv.at[r, 0], ydev(yp))
+        push(far_b[r].at[hi], r_far[r].at[hi], p_send.at[r, 1], p_recv.at[r, 1], ydev(ym))
+
+    def scatter_mid(r):
         v = partial(yp, r)
-        plus[r, hi, :] = v[160:].astype(BF)
-        push(plus.at[r, hi], r_plus.at[r, hi], p_send.at[r, 2], p_recv.at[r, 2], ydev(yp))
+        plus[r][hi, :] = v[160:].astype(BF)
+        push(plus[r].at[hi], r_plus[r].at[hi], p_send.at[r, 2], p_recv.at[r, 2], ydev(yp))
         u = partial(ym, r)
-        minus[r, lo, :] = u[:160].astype(BF)
-        push(minus.at[r, lo], r_minus.at[r, lo], p_send.at[r, 3], p_recv.at[r, 3], ydev(ym))
+        minus[r][lo, :] = u[:160].astype(BF)
+        push(minus[r].at[lo], r_minus[r].at[lo], p_send.at[r, 3], p_recv.at[r, 3], ydev(ym))
         kept[r] = v[:160], u[160:]
 
     def scatter_near(r):
         v, u = kept[r]
-        landed(r_far.at[r, lo], p_recv.at[r, 0])
-        plus[r, lo, :] = (v + r_far[r, lo, :].astype(F32)).astype(BF)
-        push(plus.at[r, lo], r_plus.at[r, lo], p_send.at[r, 4], p_recv.at[r, 4], ydev(yp))
-        landed(r_far.at[r, hi], p_recv.at[r, 1])
-        minus[r, hi, :] = (u + r_far[r, hi, :].astype(F32)).astype(BF)
-        push(minus.at[r, hi], r_minus.at[r, hi], p_send.at[r, 5], p_recv.at[r, 5], ydev(ym))
+        landed(r_far[r].at[lo], p_recv.at[r, 0])
+        plus[r][lo, :] = (v + r_far[r][lo, :].astype(F32)).astype(BF)
+        push(plus[r].at[lo], r_plus[r].at[lo], p_send.at[r, 4], p_recv.at[r, 4], ydev(yp))
+        landed(r_far[r].at[hi], p_recv.at[r, 1])
+        minus[r][hi, :] = (u + r_far[r][hi, :].astype(F32)).astype(BF)
+        push(minus[r].at[hi], r_minus[r].at[hi], p_send.at[r, 5], p_recv.at[r, 5], ydev(ym))
 
     def keep(r):
-        cols = pl.ds(r * half, half)
+        cols = pl.ds(*parts[r])
         res[pl.ds(0, 320), cols] = partial(y, r) + res[pl.ds(pl.multiple_of(64 * hl, 64), 320), cols]
 
     def finish(r):
         for sl, k1, k2 in ((hi, 2, 5), (lo, 4, 3)):
-            landed(r_plus.at[r, sl], p_recv.at[r, k1])
-            landed(r_minus.at[r, sl], p_recv.at[r, k2])
-        cols = pl.ds(r * half, half)
-        out[:, cols] = (res[pl.ds(0, 320), cols] + r_plus[r].astype(F32) + r_minus[r].astype(F32)).astype(BF)
+            landed(r_plus[r].at[sl], p_recv.at[r, k1])
+            landed(r_minus[r].at[sl], p_recv.at[r, k2])
+        cols = pl.ds(*parts[r])
+        out[:, cols] = (res[pl.ds(0, 320), cols] + r_plus[r][...].astype(F32) + r_minus[r][...].astype(F32)).astype(BF)
 
     scatter_far(0)
+    scatter_mid(0)
     keep(0)
+    fwd_c(2)
+    fwd_c(3)
     scatter_near(0)
-    fwd_c(1)
     scatter_far(1)
+    scatter_far(2)
+    scatter_mid(1)
+    scatter_mid(2)
+    scatter_near(1)
     keep(1)
-    scatter_near(1)
+    scatter_near(2)
+    keep(2)
     finish(0)
     finish(1)
+    finish(2)
 
     for k in range(1, 16):
         landed(q_land(0), a_send.at[0, k])
@@ -534,13 +581,14 @@
         def _():
             landed(land_o.at[k], o_send.at[k])
 
-        landed(at(0, 0), c_send.at[0, k])
-        landed(at(0, 0), c_send.at[1, k])
-        landed(at(0, 0), c_send.at[2, k])
+    for k in range(8):
+        for i in range(3):
+            landed(at(0, 0), c_send.at[i, k])
     for r in range(2):
         landed(kv_at(0, r), e_send.at[r])
+    for r in range(3):
         for k in range(6):
-            landed(far_b.at[0, lo], p_send.at[r, k])
+            landed(far_b[r].at[lo], p_send.at[r, k])
     main.drain()
     outw.drain()
     keys.drain()
@@ -560,7 +608,7 @@
             VM((TOK, D), BF),
             VM((256, ROWS, TOK), F32),
             VM((640, TOK), F32),
-            VM((TOK, D), BF),
+            VM((TOK, 640), BF),
             VM((16, ROWS, WC), BF),
             VM((80, WC), F32),
             VM((16, 320, WC), BF),
@@ -578,11 +626,12 @@
             VM((2, TOK, 256), F32),
             VM((4, TOK, 256), BF),
         ]
-        + [VM((2, 320, 256), BF)] * 6
+        + [VM((320, 256), BF)] * 6
+        + [VM((2, 320, 128), BF)] * 6
         + [
             DMA((2, 16)), DMA((2, 16)), DMA((4,)), DMA((4,)), DMA((16,)), DMA((16,)),
             DMA((sends_of(4),)), DMA((16, 4)), DMA((sends_of(2),)), DMA((16, 2)), DMA((sends_of(4),)), DMA((16, 4)), DMA((2,)),
-            DMA((3, 4)), DMA((4, 4)), DMA((2, 6)), DMA((2, 6)), DMA,
+            DMA((3, 8)), DMA((4, 8)), DMA((3, 6)), DMA((3, 6)), DMA,
             VM((D,), BF), VM((4096,), BF), VM((2048,), BF), VM((1, TOK), jnp.int32), VM((1, TOK), jnp.int32), VM((HD // 2, TOK), F32), VM((1, D), F32),
             DMA((6,)),
         ],

time: 111 us -> 105 us (0.946)
  Pallas kernels: 109 us -> 103 us
    pallas_call x1, Pallas kernels: 109 us -> 103 us  [per_device(): pl.pallas_call(layer, out_shape=jax.ShapeDtypeStruct((320, TOK), BF), in_...]
where the time goes in v4:
time: 105 us
  Pallas kernels  103 us (98%)
  local copies, waits for them, and re-layouts  1.72 us (2%)
    pallas_call x1, Pallas kernels, per_device(): pl.pallas_call(layer, out_shape=jax.ShapeDtypeStruct((320, TOK), BF), in_...  103 us

profile of v4, /device:TPU:6, one launch (start us, length us, event | category | flops | bytes accessed | tf_op | source)
XLA Modules:
  0.0 104.7 jit_solution(1115622374778147384)
XLA Ops:
  0.0 102.9 %layer.1 = bf16[320,512]{1,0:T(8,128)(2,1)} custom-call(s32[256]{0:T(256)} %dm.1, bf16[512,5120]{1,0:T(8,128)(2,1)} %x_hbm.1, bf16[20,4096]{1,0:T(8,128)(2,1)} %wq.1, bf16[20,2048]{1,0:T(8,128)(2,1)} %wkv.1, bf16[20,4096]{1,0:T(8,128)(2,1)} %bitcast.5, bf16[5120]{0:T(1024)(128)(2,1)} %gain_h.1, bf16[4096]{0:T(1024)(128)(2,1)} %qb_h.1, bf16[2048]{0:T(1024)(128)(2,1)} %kb_h.1, ...), custom_call_target="tpu_custom_call" | custom-call | tf_op jit(solution)/shard_map/layer/pallas_call | solution.py:602
  102.9 1.7 %copy.13 = bf16[512,320]{0,1:T(8,128)(2,1)} copy(bf16[512,320]{0,1:T(8,128)(2,1)} %bitcast.4) | data formatting | bytes 655360

commit v5 on v4

--- a/solution.py
+++ b/solution.py
@@ -325,19 +325,14 @@
     main.zfwd(0)
     group(3)
     group(2)
-    send_segs()
-    send_out()
     acc_w[...] = jnp.zeros((TOK, WC), F32)
 
-    for k in (1, 2, 3, 5):
-        in_copy[k].wait()
-    angle = freq[...] * pos[...].astype(F32)
-    cos_t, sin_t = cos_sin(angle)
-    trig[0] = jnp.concatenate([cos_t, cos_t], axis=0).T
-    trig[1] = jnp.concatenate([-sin_t, sin_t], axis=0).T
-    window = pl.ds(pl.multiple_of(128 * ((5 * t) // 2), 128), 384)
-    res[...] = xv[:, window].astype(F32).T
-
+    def rope_tables():
+        for k in (1, 2, 3, 5):
+            in_copy[k].wait()
+        cos_t, sin_t = cos_sin(freq[...] * pos[...].astype(F32))
+        trig[0] = jnp.concatenate([cos_t, cos_t], axis=0).T
+        trig[1] = jnp.concatenate([-sin_t, sin_t], axis=0).T
 
     def mul(i):
         pair = pick(main.order, i) // 2
@@ -346,11 +341,11 @@
 
     run(8, mul, {
         0: seq((main.side, False, 0), (main.zfwd, 1), (main.sibs, 0)),
-        1: seq((main.zfwd, 3), (main.zfwd, 2), (main.side, False, 1), (main.sibs, 1)),
-        2: seq((main.side, True, 0), (main.side, False, 3), (main.side, False, 2), (main.sibs, 2)),
+        1: seq((rope_tables,), (main.side, False, 1), (main.zfwd, 3), (main.zfwd, 2), (main.sibs, 1)),
+        2: seq((send_segs,), (send_out,), (main.side, True, 0), (main.side, False, 3), (main.side, False, 2), (main.sibs, 2)),
         3: seq((main.far, False, 0), (main.side, True, 1), (main.sibs, 3)),
         4: seq((main.far, False, 1), (main.side, True, 3), (main.side, True, 2), (main.sibs, 4)),
-        5: seq((main.far, False, 3), (main.far, False, 2), (squeeze_out,), (main.sibs, 5)),
+        5: seq((main.far, False, 3), (main.far, False, 2), (main.sibs, 5)),
         6: seq((main.far, True, 0), (main.far, True, 1), (main.sibs, 6)),
         7: seq((main.far, True, 3), (main.far, True, 2), (main.sibs, 7)),
     })
@@ -394,6 +389,9 @@
         return carry
 
     lax.fori_loop(0, 16, column, 0)
+    squeeze_out()
+    window = pl.ds(pl.multiple_of(128 * ((5 * t) // 2), 128), 384)
+    res[...] = xv[:, window].astype(F32).T
 
     def block(pair, r, first):
         ss = []
@@ -481,14 +479,13 @@
 
     run(6, double, {
         0: seq((keys.side, True, 2), (keys.far, False, 0, 1), (keys.sibs, 2), (keys.sibs, 3)),
-        1: seq((keys.side, True, 3), (keys.far, False, 2, 3), (keys.far, True, 0), (keys.sibs, 4), (keys.sibs, 5)),
-        2: seq((keys.far, True, 1, 2, 3), (outw.z_in, 0, 1), (outw.own_x, 0, 1), (outw.z_out, 0, 1), (keys.sibs, 6), (keys.sibs, 7)),
+        1: seq((keys.side, True, 3), (outw.own_x, 0, 1), (keys.far, False, 2, 3), (keys.far, True, 0), (keys.sibs, 4), (keys.sibs, 5)),
+        2: seq((outw.z_in, 0, 1), (outw.z_out, 0, 1), (keys.far, True, 1, 2, 3), (keys.sibs, 6), (keys.sibs, 7)),
         3: seq((mine_c, 0),),
         4: seq((outw.side, False, 0, 1)),
-        5: seq((fwd_c, 0), (outw.side, True, 0, 1)),
+        5: seq((outw.side, True, 0, 1), (fwd_c, 0, 1)),
     })
     mine_c(1)
-    fwd_c(1)
     outw.far(False, 0, 1)
     outw.far(True, 0, 1)
     for k in range(8):

time: 105 us -> 104 us (level); the launches traced: 105 us -> 102 us
  Pallas kernels: 103 us -> 100 us
    pallas_call x1, Pallas kernels: 103 us -> 100 us  [per_device(): pl.pallas_call(layer, out_shape=jax.ShapeDtypeStruct((320, TOK), BF), in_...]
where the time goes in v5:
time: 104 us; the launch traced here: 102 us
  Pallas kernels  100 us (96%)
  local copies, waits for them, and re-layouts  1.72 us (2%)
    pallas_call x1, Pallas kernels, per_device(): pl.pallas_call(layer, out_shape=jax.ShapeDtypeStruct((320, TOK), BF), in_...  100 us

profile of v5, /device:TPU:6, one launch (start us, length us, event | category | flops | bytes accessed | tf_op | source)
XLA Modules:
  0.0 102.1 jit_solution(8005832154400975063)
XLA Ops:
  0.0 100.3 %layer.1 = bf16[320,512]{1,0:T(8,128)(2,1)} custom-call(s32[256]{0:T(256)} %dm.1, bf16[512,5120]{1,0:T(8,128)(2,1)} %x_hbm.1, bf16[20,4096]{1,0:T(8,128)(2,1)} %wq.1, bf16[20,2048]{1,0:T(8,128)(2,1)} %wkv.1, bf16[20,4096]{1,0:T(8,128)(2,1)} %bitcast.5, bf16[5120]{0:T(1024)(128)(2,1)} %gain_h.1, bf16[4096]{0:T(1024)(128)(2,1)} %qb_h.1, bf16[2048]{0:T(1024)(128)(2,1)} %kb_h.1, ...), custom_call_target="tpu_custom_call" | custom-call | tf_op jit(solution)/shard_map/layer/pallas_call | solution.py:599
  100.4 1.7 %copy.13 = bf16[512,320]{0,1:T(8,128)(2,1)} copy(bf16[512,320]{0,1:T(8,128)(2,1)} %bitcast.4) | data formatting | bytes 655360

commit v6 on v5

--- a/solution.py
+++ b/solution.py
@@ -199,7 +199,7 @@
         lane = pl.multiple_of(128 * ((hl + p // 2) % 2), 128)
         return kvg.at[k, pl.ds(256 * (p % 2), 256), pl.ds(lane, 128)]
 
-    keys = Gather(kv_at, 4, k_send, k_recv)
+    keys = Gather(kv_at, 4, k_send, k_recv, (3,))
     tgt_blk = blk_of(x, y // 2, y % 2)
     tgt_tp = [yb * 4 + 2 * zl + c for yb in range(4)]
     src_blk = blk_of(x, zh // 2, zh % 2)

time: 104 us -> 103 us (level); the launches traced: 102 us -> 103 us
  Pallas kernels: 100 us -> 102 us
    pallas_call x1, Pallas kernels: 100 us -> 102 us  [per_device(): pl.pallas_call(layer, out_shape=jax.ShapeDtypeStruct((320, TOK), BF), in_...]
where the time goes in v6:
time: 103 us
  Pallas kernels  102 us (99%)
  local copies, waits for them, and re-layouts  1.72 us (2%)
    pallas_call x1, Pallas kernels, per_device(): pl.pallas_call(layer, out_shape=jax.ShapeDtypeStruct((320, TOK), BF), in_...  102 us

profile of v6, /device:TPU:6, one launch (start us, length us, event | category | flops | bytes accessed | tf_op | source)
XLA Modules:
  0.0 103.3 jit_solution(15425948617771731217)
XLA Ops:
  0.0 101.5 %layer.1 = bf16[320,512]{1,0:T(8,128)(2,1)} custom-call(s32[256]{0:T(256)} %dm.1, bf16[512,5120]{1,0:T(8,128)(2,1)} %x_hbm.1, bf16[20,4096]{1,0:T(8,128)(2,1)} %wq.1, bf16[20,2048]{1,0:T(8,128)(2,1)} %wkv.1, bf16[20,4096]{1,0:T(8,128)(2,1)} %bitcast.5, bf16[5120]{0:T(1024)(128)(2,1)} %gain_h.1, bf16[4096]{0:T(1024)(128)(2,1)} %qb_h.1, bf16[2048]{0:T(1024)(128)(2,1)} %kb_h.1, ...), custom_call_target="tpu_custom_call" | custom-call | tf_op jit(solution)/shard_map/layer/pallas_call | solution.py:599
  101.5 1.7 %copy.13 = bf16[512,320]{0,1:T(8,128)(2,1)} copy(bf16[512,320]{0,1:T(8,128)(2,1)} %bitcast.4) | data formatting | bytes 655360
